TPU v7x, 32 devices: a whole 2x2x4 slice. The times are simulated.
32 devices in a mesh: section: 8 (over z, y), tensor: 4 (over x, core).
Axes of the slice: x: 2, y: 2, z: 4, core: 2. Of those that a mesh axis runs over, the one named last changes fastest.
Arguments:
- section_input: bfloat16 [8, 512, 4096], P('section', 'tensor'), may hold values from -6 to 6
- history: bfloat16 [8, 1, 512, 4096], P('section', None, 'tensor'), may hold values from -6 to 6
- query_weight: bfloat16 [8, 4096, 3072], P('section', None, 'tensor'), may hold values from -0.4 to 0.4
- key_weight: bfloat16 [8, 4096, 512], P('section', None, 'tensor'), may hold values from -0.4 to 0.4
- value_weight: bfloat16 [8, 4096, 512], P('section', None, 'tensor'), may hold values from -0.09375 to 0.09375
- output_weight: bfloat16 [8, 3072, 4096], P('section', 'tensor'), may hold values from -0.5 to 0.5
- mix_weights: float32 [8, 2], replicated, may hold values from 0.2 to 0.6
Outputs:
- next_input: bfloat16 [8, 512, 4096], P('section', 'tensor')
All inputs are finite; a program needn't handle non-finite values.
Results may differ from a plain program's by a relative error of at most 0.013.
The roundings to bfloat16 on the way count: a program that leaves them out, or rounds other values in their place, can miss the bound.
Values may be sent and summed in bfloat16 or wider, within the bound.
A program may use at most 128 MiB of HBM per device.

v0:
```python
import functools
import math

import jax
import jax.numpy as jnp
from jax import lax
from jax.experimental import pallas as pl
from jax.experimental.pallas import tpu as pltpu
from jax.sharding import PartitionSpec as P

HEAD_DIM = 64
DILATION_STRIDE = 4
MESH = pl.DeviceIdType.MESH
LAG = 2


def start(copy):
    copy.start()
    return copy


def tick_kernel(
    sections,
    x_hbm,
    hist_hbm,
    wq_hbm,
    wk_hbm,
    wv_hbm,
    wo_hbm,
    mix_hbm,
    out_hbm,
    x_own,
    chip_rows,
    peer_rows,
    w_all,
    w_out,
    q_all,
    k_pad,
    v_pad,
    peer_heads,
    own_heads,
    peer_keep,
    peer_give,
    peer_got,
    own_parts,
    own_got,
    x_in,
    mixed,
    hist_in,
    mix_v,
    w_sem,
    wo_sem,
    x_sem,
    mix_sem,
    hist_s,
    hist_r,
    sib_s,
    sib_r,
    gx_s,
    gx_r,
    fw_s,
    fw_r,
    ps_s,
    ps_r,
    os_s,
    os_r,
    xs_s,
    xs_r,
    out_s,
    out_r,
    block_in,
    store_sem,
):
    section = lax.axis_index("section")
    me = lax.axis_index("tensor")
    hi, lo = me // 2, me % 2
    sibling = hi * 2 + (1 - lo)
    peer = (1 - hi) * 2 + lo
    rows, width = x_own.shape
    slots = hist_in.shape[0]
    piece = rows // 2
    q_tiles = w_all.shape[0] - 1
    tile = w_all.shape[2]
    half = tile // 2
    col_chunks, _, cols = w_out.shape
    side = col_chunks // 2
    nxt = lax.rem(section + 1, sections)
    prv = lax.rem(section + sections - 1, sections)

    load_x = start(pltpu.make_async_copy(x_hbm.at[0], x_own, x_sem))
    barrier = pltpu.get_barrier_semaphore()
    for other in (sibling, peer, (1 - hi) * 2 + (1 - lo)):
        pl.semaphore_signal(barrier, inc=1, device_id={"tensor": other}, device_id_type=MESH)
    for other in (nxt, prv):
        pl.semaphore_signal(barrier, inc=1, device_id={"section": other}, device_id_type=MESH)
    expected = jnp.int32(5)
    for k in range(1, slots + 1):
        step = DILATION_STRIDE * k
        forward, backward = section + step < sections, prv >= step

        @pl.when(forward)
        def _():
            pl.semaphore_signal(
                barrier,
                inc=1,
                device_id={"section": lax.rem(section + step + 1, sections)},
                device_id_type=MESH,
            )

        @pl.when(backward)
        def _():
            pl.semaphore_signal(
                barrier, inc=1, device_id={"section": prv - step}, device_id_type=MESH
            )

        expected = expected + forward.astype(jnp.int32) + backward.astype(jnp.int32)

    loads = []
    for j in range(q_tiles):
        loads.append(
            pltpu.make_async_copy(
                wq_hbm.at[0, :, pl.ds(j * tile, tile)], w_all.at[j], w_sem.at[j]
            )
        )
    loads.append(
        pltpu.make_async_copy(
            wk_hbm.at[0], w_all.at[q_tiles, :, pl.ds(0, half)], w_sem.at[q_tiles]
        )
    )
    loads.append(
        pltpu.make_async_copy(
            wv_hbm.at[0], w_all.at[q_tiles, :, pl.ds(half, half)], w_sem.at[q_tiles + 1]
        )
    )
    load_x.wait()
    for copy in loads:
        copy.start()
    load_mix = start(pltpu.make_async_copy(mix_hbm, mix_v, mix_sem))
    mine = pl.multiple_of(lo * rows, rows)

    def norm_rows(i, carry):
        at = pl.multiple_of(i * 16, 16)
        values = x_own[pl.ds(at, 16), :].astype(jnp.float32)
        inv = lax.rsqrt(jnp.mean(values * values, axis=-1, keepdims=True) + 1e-05)
        chip_rows[pl.ds(pl.multiple_of(mine + at, 16), 16), :] = (values * inv).astype(jnp.bfloat16)
        return carry

    lax.fori_loop(0, rows // 16, norm_rows, 0)
    pl.semaphore_wait(barrier, expected)

    def gather_copy(j):
        return pltpu.make_async_remote_copy(
            src_ref=chip_rows.at[pl.ds(pl.multiple_of(j * rows + lo * piece, piece), piece)],
            dst_ref=peer_rows.at[j, pl.ds(pl.multiple_of(lo * piece, piece), piece)],
            send_sem=gx_s.at[j],
            recv_sem=gx_r.at[j],
            device_id={"tensor": peer},
            device_id_type=MESH,
        )

    def forward_copy(j):
        place = peer_rows.at[j, pl.ds(pl.multiple_of(lo * piece, piece), piece)]
        return pltpu.make_async_remote_copy(
            src_ref=place,
            dst_ref=place,
            send_sem=fw_s.at[j],
            recv_sem=fw_r.at[j],
            device_id={"tensor": sibling},
            device_id_type=MESH,
        )

    def sibling_copy(i):
        which = 1 - lo if i == 0 else lo
        place = chip_rows.at[pl.ds(pl.multiple_of(mine + which * piece, piece), piece)]
        return pltpu.make_async_remote_copy(
            src_ref=place,
            dst_ref=place,
            send_sem=sib_s.at[i],
            recv_sem=sib_r.at[i],
            device_id={"tensor": sibling},
            device_id_type=MESH,
        )

    @pl.when(lo == 0)
    def _():
        gather_copy(0).start()

    for i in range(2):
        sibling_copy(i).start()
    sibling_copy(0).wait_recv()

    @pl.when(lo == 1)
    def _():
        gather_copy(0).start()

    gather_copy(1).start()

    def hist_copy(k):
        return pltpu.make_async_remote_copy(
            src_ref=hist_hbm.at[0, k - 1],
            dst_ref=hist_in.at[k - 1],
            send_sem=hist_s.at[k - 1],
            recv_sem=hist_r.at[k - 1],
            device_id={"section": lax.rem(section + DILATION_STRIDE * k + 1, sections)},
            device_id_type=MESH,
        )

    for k in range(1, slots + 1):
        step = DILATION_STRIDE * k

        @pl.when(section + step < sections)
        def _():
            hist_copy(k).start()

        @pl.when(prv < step)
        def _():
            hist_in[k - 1] = jnp.zeros((rows, width), hist_in.dtype)

    out_loads = []
    for c in range(col_chunks):
        out_loads.append(
            start(
                pltpu.make_async_copy(
                    wo_hbm.at[0, :, pl.ds(c * cols, cols)], w_out.at[c], wo_sem.at[c]
                )
            )
        )

    scale = 1.0 / math.sqrt(HEAD_DIM)

    def project_query(rows_ref, target):
        size = rows_ref.shape[0]
        where = pl.ds(pl.multiple_of(target, size), size)

        def q_tile(j, carry):
            acc = jnp.dot(rows_ref[...], w_all[j], preferred_element_type=jnp.float32)
            acc = acc.astype(jnp.bfloat16) * jnp.bfloat16(scale)
            q_all[2 * j, where, :] = acc[:, :half]
            q_all[2 * j + 1, where, :] = acc[:, half:]
            return carry

        lax.fori_loop(0, q_tiles, q_tile, 0)

    def project_key_value(rows_ref, target):
        size = rows_ref.shape[0]
        where = pl.ds(pl.multiple_of(target, size), size)
        acc = jnp.dot(rows_ref[...], w_all[q_tiles], preferred_element_type=jnp.float32)
        acc = acc.astype(jnp.bfloat16).astype(jnp.float32)
        for part, padded in ((acc[:, :half], k_pad), (acc[:, half:], v_pad)):
            lane = lax.broadcasted_iota(jnp.int32, part.shape, 1)
            turned = pltpu.roll(part, HEAD_DIM, 1)
            low = lane < HEAD_DIM
            zero = jnp.zeros_like(part)
            forms = (
                jnp.where(low, part, zero),
                jnp.where(low, zero, turned),
                jnp.where(low, turned, zero),
                jnp.where(low, zero, part),
            )
            for f, form in enumerate(forms):
                padded[f, where, :] = form.astype(jnp.bfloat16)

    pairs = q_all.shape[0]
    pairs_per_kv = pairs // (half // HEAD_DIM)

    def attend(heads_ref, first, size, keys):
        def pair(p, carry):
            query = q_all[p, first : first + size, :]
            row_at = first + lax.broadcasted_iota(jnp.int32, (size, keys), 0)
            key_at = lax.broadcasted_iota(jnp.int32, (size, keys), 1)
            seen = row_at >= key_at
            kv = p // pairs_per_kv
            total = None
            for which in range(2):
                scores = lax.dot_general(
                    query,
                    k_pad[kv * 2 + which, :keys, :],
                    (((1,), (1,)), ((), ())),
                    preferred_element_type=jnp.float32,
                )
                scores = jnp.where(seen, scores, -1e30)
                top = jnp.max(scores, axis=-1, keepdims=True)
                weights = jnp.exp(scores - top)
                weights = weights * (1.0 / jnp.sum(weights, axis=-1, keepdims=True))
                term = jnp.dot(
                    weights.astype(jnp.bfloat16),
                    v_pad[kv * 2 + which, :keys, :],
                    preferred_element_type=jnp.float32,
                )
                total = term if total is None else total + term
            heads_ref[:, pl.ds(pl.multiple_of(p * half, half), half)] = total.astype(jnp.bfloat16)
            return carry

        lax.fori_loop(0, pairs, pair, 0)

    def give_copy(j, i):
        return pltpu.make_async_remote_copy(
            src_ref=peer_give.at[j, i],
            dst_ref=peer_got.at[j, i],
            send_sem=ps_s.at[j, i],
            recv_sem=ps_r.at[j, i],
            device_id={"tensor": sibling},
            device_id_type=MESH,
        )

    def cross_copy(j, i):
        return pltpu.make_async_remote_copy(
            src_ref=peer_keep.at[j, i],
            dst_ref=x_in.at[lo * side + i],
            send_sem=xs_s.at[j, i],
            recv_sem=xs_r.at[lo * side + i],
            device_id={"tensor": (1 - hi) * 2 + j},
            device_id_type=MESH,
        )

    def cross_arrival(c):
        return pltpu.make_async_remote_copy(
            src_ref=x_in.at[c],
            dst_ref=x_in.at[c],
            send_sem=xs_s.at[0, 0],
            recv_sem=xs_r.at[c],
            device_id={"tensor": peer},
            device_id_type=MESH,
        )

    def peer_output(j):
        def part(c):
            acc = jnp.dot(peer_heads[j], w_out[c], preferred_element_type=jnp.float32)
            return acc.astype(jnp.bfloat16)

        def step(i, carry):
            @pl.when(i < side)
            def _():
                peer_give[j, i] = part((1 - lo) * side + i)
                peer_keep[j, i] = part(lo * side + i)
                give_copy(j, i).start()

            @pl.when(i >= LAG)
            def _():
                at = i - LAG
                give_copy(j, at).wait_recv()
                total = peer_keep[j, at].astype(jnp.float32) + peer_got[j, at].astype(jnp.float32)
                peer_keep[j, at] = total.astype(jnp.bfloat16)
                cross_copy(j, at).start()

            return carry

        lax.fori_loop(0, side + LAG, step, 0)

    def own_copy(c):
        return pltpu.make_async_remote_copy(
            src_ref=own_parts.at[c, 1 - lo],
            dst_ref=own_got.at[c],
            send_sem=os_s.at[c],
            recv_sem=os_r.at[c],
            device_id={"tensor": sibling},
            device_id_type=MESH,
        )

    def own_part(c):
        acc = jnp.dot(own_heads[...], w_out[c], preferred_element_type=jnp.float32)
        acc = acc.astype(jnp.bfloat16)
        own_parts[c, 0] = acc[:rows]
        own_parts[c, 1] = acc[rows:]
        own_copy(c).start()

    def out_copy(c):
        return pltpu.make_async_remote_copy(
            src_ref=mixed.at[c],
            dst_ref=block_in.at[c],
            send_sem=out_s.at[c],
            recv_sem=out_r.at[c],
            device_id={"section": nxt},
            device_id_type=MESH,
        )

    for copy in loads:
        copy.wait()
    sibling_copy(1).wait_recv()
    project_key_value(chip_rows, hi * 2 * rows)
    project_query(chip_rows, hi * 2 * rows)
    for copy in out_loads:
        copy.wait()
    load_mix.wait()

    @pl.when(hi == 0)
    def _():
        attend(own_heads, 0, 2 * rows, 2 * rows)

        def own_step(c, carry):
            own_part(c)
            return carry

        lax.fori_loop(0, col_chunks, own_step, 0)

    def final_chunk(c):
        own_copy(c).wait_recv()
        total = own_parts[c, lo].astype(jnp.float32) + own_got[c].astype(jnp.float32)
        where = pl.ds(pl.multiple_of(c * cols, cols), cols)
        cross_arrival(c).wait_recv()
        total = total + x_in[c].astype(jnp.float32)
        block = (x_own[:, where].astype(jnp.float32) + total).astype(jnp.bfloat16)
        mixed[c] = block
        out_copy(c).start()

    def column(i):
        return (i % 2) * side + i // 2

    def finish():
        def final_step(i, carry):
            final_chunk(column(i))
            return carry

        lax.fori_loop(0, col_chunks, final_step, 0)

    def peer_queries(j):
        project_query(peer_rows.at[j], ((1 - hi) * 2 + j) * rows)

        @pl.when(hi == 0)
        def _():
            attend(peer_heads.at[j], (2 + j) * rows, rows, (3 + j) * rows)

        @pl.when(hi == 1)
        def _():
            attend(peer_heads.at[j], j * rows, rows, (1 + j) * rows)

        if j == 1:

            @pl.when((hi == 0) & (lo == 0))
            def _():
                finish()

        peer_output(j)

    for j in range(2):
        gather_copy(j).wait_recv()
        forward_copy(j).start()
        forward_copy(j).wait_recv()
        project_key_value(peer_rows.at[j], ((1 - hi) * 2 + j) * rows)
        if j == 0:
            peer_queries(j)

    @pl.when(hi == 1)
    def _():
        attend(own_heads, 2 * rows, 2 * rows, 4 * rows)

        def own_step(i, carry):
            own_part(column(i))

            @pl.when((lo == 0) & (i >= LAG))
            def _():
                final_chunk(column(i - LAG))

            return carry

        lax.fori_loop(0, col_chunks, own_step, 0)

        @pl.when(lo == 0)
        def _():
            for i in range(col_chunks - LAG, col_chunks):
                final_chunk(column(i))

    peer_queries(1)

    @pl.when(lo == 1)
    def _():
        finish()

    for k in range(1, slots + 1):

        @pl.when(prv >= DILATION_STRIDE * k)
        def _():
            hist_copy(k).wait_recv()

    def store_copy(c):
        return pltpu.make_async_copy(
            block_in.at[c],
            out_hbm.at[0, :, pl.ds(pl.multiple_of(c * cols, cols), cols)],
            store_sem.at[c],
        )

    def mix_step(i, carry):
        c = column(i)
        out_copy(c).wait_recv()
        where = pl.ds(pl.multiple_of(c * cols, cols), cols)
        factors = mix_v[pl.ds(prv, 1), :]
        value = factors[:, 0:1] * block_in[c].astype(jnp.float32)
        for k in range(1, slots + 1):
            past = hist_in[k - 1, :, where].astype(jnp.float32)
            value = value + factors[:, k : k + 1] * past
        block_in[c] = value.astype(jnp.bfloat16)
        store_copy(c).start()
        return carry

    lax.fori_loop(0, col_chunks, mix_step, 0)

    for i in range(2):
        sibling_copy(i).wait_send()
        gather_copy(i).wait_send()
        forward_copy(i).wait_send()
    for k in range(1, slots + 1):

        @pl.when(section + DILATION_STRIDE * k < sections)
        def _():
            hist_copy(k).wait_send()

    def drain(c, carry):
        j, i = c // side, c % side
        give_copy(j, i).wait_send()
        cross_copy(j, i).wait_send()
        own_copy(c).wait_send()
        out_copy(c).wait_send()
        store_copy(c).wait()
        return carry

    lax.fori_loop(0, col_chunks, drain, 0)


def solution(mesh):
    sections, tensor = mesh.shape["section"], mesh.shape["tensor"]
    assert tensor == 4
    col_chunks = 8

    def on_device(x, history, wq, wk, wv, wo, mix_weights):
        rows, width = x.shape[1:]
        slots = history.shape[1]
        q_width, kv_width = wq.shape[2], wk.shape[2]
        seq = rows * tensor
        tile = 2 * kv_width
        q_tiles = q_width // tile
        cols = width // col_chunks
        bf16 = jnp.bfloat16
        dma = pltpu.SemaphoreType.DMA
        hbm = pl.BlockSpec(memory_space=pl.ANY)
        return pl.pallas_call(
            functools.partial(tick_kernel, sections),
            out_shape=jax.ShapeDtypeStruct(x.shape, bf16),
            in_specs=[hbm] * 7,
            out_specs=hbm,
            scratch_shapes=[
                pltpu.VMEM((rows, width), bf16),
                pltpu.VMEM((2 * rows, width), bf16),
                pltpu.VMEM((2, rows, width), bf16),
                pltpu.VMEM((q_tiles + 1, width, tile), bf16),
                pltpu.VMEM((col_chunks, q_width, cols), bf16),
                pltpu.VMEM((2 * q_tiles, seq, kv_width), bf16),
                pltpu.VMEM((4, seq, kv_width), bf16),
                pltpu.VMEM((4, seq, kv_width), bf16),
                pltpu.VMEM((2, rows, q_width), bf16),
                pltpu.VMEM((2 * rows, q_width), bf16),
                pltpu.VMEM((2, col_chunks // 2, rows, cols), bf16),
                pltpu.VMEM((2, col_chunks // 2, rows, cols), bf16),
                pltpu.VMEM((2, col_chunks // 2, rows, cols), bf16),
                pltpu.VMEM((col_chunks, 2, rows, cols), bf16),
                pltpu.VMEM((col_chunks, rows, cols), bf16),
                pltpu.VMEM((col_chunks, rows, cols), bf16),
                pltpu.VMEM((col_chunks, rows, cols), bf16),
                pltpu.VMEM((slots, rows, width), bf16),
                pltpu.VMEM(mix_weights.shape, mix_weights.dtype),
                dma((q_tiles + 2,)),
                dma((col_chunks,)),
                dma,
                dma,
                dma((slots,)),
                dma((slots,)),
                dma((2,)),
                dma((2,)),
                dma((2,)),
                dma((2,)),
                dma((2,)),
                dma((2,)),
                dma((2, col_chunks // 2)),
                dma((2, col_chunks // 2)),
                dma((col_chunks,)),
                dma((col_chunks,)),
                dma((2, col_chunks // 2)),
                dma((col_chunks,)),
                dma((col_chunks,)),
                dma((col_chunks,)),
                pltpu.VMEM((col_chunks, rows, cols), bf16),
                dma((col_chunks,)),
            ],
            compiler_params=pltpu.CompilerParams(
                collective_id=0, has_side_effects=True, vmem_limit_bytes=60 * 1024 * 1024
            ),
        )(x, history, wq, wk, wv, wo, mix_weights)

    placed = (
        P("section", "tensor", None),
        P("section", None, "tensor", None),
        P("section", None, "tensor"),
        P("section", None, "tensor"),
        P("section", None, "tensor"),
        P("section", "tensor", None),
        P(),
    )
    return jax.shard_map(
        on_device,
        mesh=mesh,
        in_specs=placed,
        out_specs=P("section", "tensor", None),
        check_vma=False,
    )
```

profile of v0, /device:TPU:31, one launch (start us, length us, event | category | flops | bytes accessed | tf_op | source)
XLA Modules:
  0.0 79.5 jit_solution(10956975017258019827)
XLA Ops:
  0.0 1.3 %copy.8.mix_hbm = f32[8,2]{1,0:T(8,128)} copy(f32[8,2]{0,1:T(2,128)} %param.13) | data formatting | bytes 128 | tf_op args[6]
  1.3 75.8 %shard_map.73 = bf16[1,128,4096]{2,1,0:T(8,128)(2,1)} custom-call(bf16[1,128,4096]{2,1,0:T(8,128)(2,1)} %x_hbm.1, bf16[1,1,128,4096]{3,2,1,0:T(8,128)(2,1)} %hist_hbm.1, bf16[1,4096,768]{2,1,0:T(8,128)(2,1)} %wq_hbm.1, bf16[1,4096,128]{2,1,0:T(8,128)(2,1)} %wk_hbm.1, bf16[1,4096,128]{2,1,0:T(8,128)(2,1)} %wv_hbm.1, bf16[1,768,4096]{2,1,0:T(8,128)(2,1)} %wo_hbm.1, ...), custom_call_target="tpu_custom_call" | custom-call | tf_op jit(solution)/shard_map/pallas_call | solution.py:535
  77.2 2.3 %copy.10 = bf16[1,128,4096]{2,1,0:T(8,128)(2,1)} copy(bf16[1,128,4096]{2,1,0:T(8,128)(2,1)} %shard_map.73) | data formatting | bytes 2097152
where the time goes:
time: 79.7 us; the launch traced here: 79.5 us
  Pallas kernels  75.8 us (95%)
  local copies, waits for them, and re-layouts  3.63 us (5%)
    pallas_call x1, Pallas kernels, on_device(): pl.pallas_call(functools.partial(tick_kernel, sections), out_shape=jax.Sh...  75.8 us
    unnamed x2, local copies, waits for them, and re-layouts  3.63 us

commit v1 on v0

v1 whole, which is shorter than its diff:
```python
import functools
import math

import jax
import jax.numpy as jnp
from jax import lax
from jax.experimental import pallas as pl
from jax.experimental.pallas import tpu as pltpu
from jax.sharding import PartitionSpec as P

HEAD_DIM = 64
DILATION_STRIDE = 4
MESH = pl.DeviceIdType.MESH
UNITS = 4
DOTS = 4
CHUNKS = 8


def start(copy):
    copy.start()
    return copy


def tick_kernel(
    sections,
    x_hbm,
    hist_hbm,
    wq_hbm,
    wk_hbm,
    wv_hbm,
    wo_hbm,
    mix_hbm,
    out,
    x_own,
    x_res,
    chip_rows,
    peer_rows,
    w_all,
    w_out,
    q_all,
    k_pad,
    v_pad,
    heads,
    own_part,
    give,
    x_in,
    mixed,
    acc,
    hist_in,
    mix_v,
    w_sem,
    wo_sem,
    x_sem,
    res_sem,
    mix_sem,
    hist_s,
    hist_r,
    sib_s,
    sib_r,
    gx_s,
    gx_r,
    fw_s,
    fw_r,
    wr_s,
    wr_r,
    xr_s,
    xr_r,
    hd_s,
    hd_r,
    xs_s,
    xs_r,
    out_s,
    out_r,
):
    section = lax.axis_index("section")
    me = lax.axis_index("tensor")
    hi, lo = me // 2, me % 2
    sibling = hi * 2 + (1 - lo)
    peer = (1 - hi) * 2 + lo
    rows, width = x_own.shape
    slots = hist_in.shape[0]
    unit = rows // UNITS
    side = width // 2
    wide = side // DOTS
    cols = side // CHUNKS
    per_dot = CHUNKS // DOTS
    q_tiles = w_all.shape[0] - 1
    tile = w_all.shape[2]
    half = tile // 2
    last = sections - 1
    nxt = lax.rem(section + 1, sections)
    prv = lax.rem(section + sections - 1, sections)
    f32, bf16 = jnp.float32, jnp.bfloat16

    middle = (section > 0) & (section < last)
    gets = [middle & (section >= DILATION_STRIDE * k) for k in range(1, slots + 1)]
    gets_last = [(section == 0) & (last >= DILATION_STRIDE * k) for k in range(1, slots + 1)]
    gives = [section + DILATION_STRIDE * k < last for k in range(1, slots + 1)]
    gives_last = [section + DILATION_STRIDE * k == last for k in range(1, slots + 1)]

    load_x = start(pltpu.make_async_copy(x_hbm.at[0], x_own, x_sem))
    barrier = pltpu.get_barrier_semaphore()

    def greet(s, t):
        pl.semaphore_signal(
            barrier, inc=1, device_id={"section": s, "tensor": t}, device_id_type=MESH
        )

    greet(section, sibling)
    greet(section, peer)
    for c in range(2):
        greet(nxt, hi * 2 + c)
        greet(prv, hi * 2 + c)
    expected = jnp.int32(6)
    for k in range(1, slots + 1):
        step = DILATION_STRIDE * k

        @pl.when(gives[k - 1])
        def _():
            for c in range(2):
                greet(section + step, hi * 2 + c)

        @pl.when(gets[k - 1])
        def _():
            for c in range(2):
                greet(section - step, hi * 2 + c)

        @pl.when(gives_last[k - 1])
        def _():
            greet(0, me)

        @pl.when(gets_last[k - 1])
        def _():
            greet(last - step, me)

        expected = expected + 2 * (gives[k - 1].astype(jnp.int32) + gets[k - 1].astype(jnp.int32))
        expected = expected + gives_last[k - 1].astype(jnp.int32)
        expected = expected + gets_last[k - 1].astype(jnp.int32)

    loads = [
        pltpu.make_async_copy(
            wk_hbm.at[0], w_all.at[q_tiles, :, pl.ds(0, half)], w_sem.at[q_tiles]
        ),
        pltpu.make_async_copy(
            wv_hbm.at[0], w_all.at[q_tiles, :, pl.ds(half, half)], w_sem.at[q_tiles + 1]
        ),
    ]
    for j in range(q_tiles):
        loads.append(
            pltpu.make_async_copy(
                wq_hbm.at[0, :, pl.ds(j * tile, tile)], w_all.at[j], w_sem.at[j]
            )
        )
    load_x.wait()
    for copy in loads:
        copy.start()
    load_mix = start(pltpu.make_async_copy(mix_hbm, mix_v, mix_sem))
    mine = pl.multiple_of(lo * rows, rows)
    my_side = pl.multiple_of(lo * side, side)
    other_side = pl.multiple_of((1 - lo) * side, side)

    def norm_unit(u):
        def norm_rows(i, carry):
            at = pl.multiple_of(u * unit + i * 16, 16)
            values = x_own[pl.ds(at, 16), :].astype(f32)
            inv = lax.rsqrt(jnp.mean(values * values, axis=-1, keepdims=True) + 1e-05)
            chip_rows[pl.ds(pl.multiple_of(mine + at, 16), 16), :] = (values * inv).astype(bf16)
            return carry

        lax.fori_loop(0, unit // 16, norm_rows, 0)

    def remote(src, dst, send, recv, s, t):
        return pltpu.make_async_remote_copy(
            src_ref=src,
            dst_ref=dst,
            send_sem=send,
            recv_sem=recv,
            device_id={"section": s, "tensor": t},
            device_id_type=MESH,
        )

    def sibling_copy(u):
        place = chip_rows.at[pl.ds(pl.multiple_of(mine + u * unit, unit), unit)]
        return remote(place, place, sib_s.at[u], sib_r.at[u], section, sibling)

    def gather_copy(j, i):
        at = (2 * i + lo) * unit
        return remote(
            chip_rows.at[pl.ds(pl.multiple_of(j * rows + at, unit), unit)],
            peer_rows.at[j, pl.ds(pl.multiple_of(at, unit), unit)],
            gx_s.at[j, i],
            gx_r.at[j, i],
            section,
            peer,
        )

    def forward_copy(j, i):
        place = peer_rows.at[j, pl.ds(pl.multiple_of((2 * i + lo) * unit, unit), unit)]
        return remote(place, place, fw_s.at[j, i], fw_r.at[j, i], section, sibling)

    norm_unit(0)
    pl.semaphore_wait(barrier, expected)
    for u in range(UNITS):
        if u > 0:
            norm_unit(u)
        sibling_copy(u).start()
        if u % 2 == 0:

            @pl.when(lo == 0)
            def _():
                gather_copy(0, u // 2).start()

    @pl.when(lo == 0)
    def _():
        for i in range(UNITS // 2):
            sibling_copy(2 * i).wait_recv()
            gather_copy(1, i).start()
        for i in range(UNITS // 2):
            sibling_copy(2 * i + 1).wait_recv()

    @pl.when(lo == 1)
    def _():
        for i in range(UNITS // 2):
            sibling_copy(2 * i + 1).wait_recv()
            gather_copy(0, i).start()
        for i in range(UNITS // 2):
            gather_copy(1, i).start()
        for i in range(UNITS // 2):
            sibling_copy(2 * i).wait_recv()

    def hist_copy(k, c, q, to_last):
        src = hist_hbm.at[0, k - 1, :, pl.ds(pl.multiple_of(c * side + q * cols, cols), cols)]
        slot = c if to_last else lo
        if to_last:
            s, t = 0, me
        else:
            s, t = section + DILATION_STRIDE * k, hi * 2 + c
        return remote(
            src,
            hist_in.at[k - 1, slot, q],
            hist_s.at[k - 1, c, q],
            hist_r.at[k - 1, slot, q],
            s,
            t,
        )

    def send_history():
        for k in range(1, slots + 1):
            for to_last, sends in ((False, gives[k - 1]), (True, gives_last[k - 1])):

                @pl.when(sends)
                def _():
                    def each(q, carry):
                        for c in range(2):
                            hist_copy(k, c, q, to_last).start()
                        return carry

                    lax.fori_loop(0, CHUNKS, each, 0)

    late = (lo == 1) & (section % 2 == 0)

    @pl.when(jnp.logical_not(late))
    def _():
        send_history()

    def weight_copy(c):
        return remote(
            wo_hbm.at[0, :, pl.ds(pl.multiple_of(other_side + c * wide, wide), wide)],
            w_out.at[lo, c],
            wr_s.at[c],
            wr_r.at[c],
            section,
            sibling,
        )

    def residual_copy():
        return remote(
            x_own.at[:, pl.ds(other_side, side)], x_res.at[lo], xr_s, xr_r, section, sibling
        )

    out_loads = []
    for c in range(DOTS):
        out_loads.append(
            start(
                pltpu.make_async_copy(
                    wo_hbm.at[0, :, pl.ds(pl.multiple_of(my_side + c * wide, wide), wide)],
                    w_out.at[lo, c],
                    wo_sem.at[c],
                )
            )
        )
        weight_copy(c).start()
    load_res = start(
        pltpu.make_async_copy(x_hbm.at[0, :, pl.ds(my_side, side)], x_res.at[lo], res_sem)
    )
    residual_copy().start()

    scale = 1.0 / math.sqrt(HEAD_DIM)

    def project_query(rows_ref, target):
        size = rows_ref.shape[0]
        where = pl.ds(pl.multiple_of(target, size), size)

        def q_tile(j, carry):
            got = jnp.dot(rows_ref[...], w_all[j], preferred_element_type=f32)
            got = got.astype(bf16) * bf16(scale)
            q_all[2 * j, where, :] = got[:, :half]
            q_all[2 * j + 1, where, :] = got[:, half:]
            return carry

        lax.fori_loop(0, q_tiles, q_tile, 0)

    def project_key_value(rows_ref, target):
        size = rows_ref.shape[0]
        where = pl.ds(pl.multiple_of(target, size), size)
        got = jnp.dot(rows_ref[...], w_all[q_tiles], preferred_element_type=f32)
        got = got.astype(bf16).astype(f32)
        for part, padded in ((got[:, :half], k_pad), (got[:, half:], v_pad)):
            lane = lax.broadcasted_iota(jnp.int32, part.shape, 1)
            turned = pltpu.roll(part, HEAD_DIM, 1)
            low = lane < HEAD_DIM
            zero = jnp.zeros_like(part)
            forms = (
                jnp.where(low, part, zero),
                jnp.where(low, zero, turned),
                jnp.where(low, turned, zero),
                jnp.where(low, zero, part),
            )
            for f, form in enumerate(forms):
                padded[f, where, :] = form.astype(bf16)

    pairs = q_all.shape[0]
    pairs_per_kv = pairs // (half // HEAD_DIM)

    def heads_copy(t):
        return remote(
            heads.at[t, lo], heads.at[t, lo], hd_s.at[t], hd_r.at[t], section, sibling
        )

    def attend(t, after=None):
        first, keys = t * rows, (t + 1) * rows

        def pair(p, carry):
            query = q_all[p, first : first + rows, :]
            row_at = first + lax.broadcasted_iota(jnp.int32, (rows, keys), 0)
            key_at = lax.broadcasted_iota(jnp.int32, (rows, keys), 1)
            seen = row_at >= key_at
            kv = p // pairs_per_kv
            total = None
            for which in range(2):
                scores = lax.dot_general(
                    query,
                    k_pad[kv * 2 + which, :keys, :],
                    (((1,), (1,)), ((), ())),
                    preferred_element_type=f32,
                )
                scores = jnp.where(seen, scores, -1e30)
                top = jnp.max(scores, axis=-1, keepdims=True)
                weights = jnp.exp(scores - top)
                weights = weights * (1.0 / jnp.sum(weights, axis=-1, keepdims=True))
                term = jnp.dot(
                    weights.astype(bf16),
                    v_pad[kv * 2 + which, :keys, :],
                    preferred_element_type=f32,
                )
                total = term if total is None else total + term
            heads[t, lo, :, pl.ds(pl.multiple_of(p * half, half), half)] = total.astype(bf16)
            if after is not None:
                after(p)
            return carry

        lax.fori_loop(0, pairs, pair, 0)
        heads_copy(t).start()

    def out_dot(t, c):
        got = jnp.dot(heads[t, 0], w_out[0, c], preferred_element_type=f32)
        return got + jnp.dot(heads[t, 1], w_out[1, c], preferred_element_type=f32)

    def cross_copy(j, q):
        return remote(give.at[j, q], x_in.at[j, q], xs_s.at[j, q], xs_r.at[j, q], section, peer)

    def peer_output(t, j, c):
        got = out_dot(t, c).astype(bf16)
        for i in range(per_dot):
            give[j, c * per_dot + i] = got[:, i * cols : (i + 1) * cols]
            cross_copy(j, c * per_dot + i).start()

    def own_output(t, j, c):
        got = out_dot(t, c)
        for i in range(per_dot):
            own_part[j, c * per_dot + i] = got[:, i * cols : (i + 1) * cols]

    def loop(count, body):
        def step(i, carry):
            body(i)
            return carry

        lax.fori_loop(0, count, step, 0)

    def out_copy(j, q):
        return remote(
            mixed.at[j, q],
            out.at[0, :, pl.ds(pl.multiple_of(my_side + q * cols, cols), cols)],
            out_s.at[j, q],
            out_r.at[lo, q],
            nxt,
            hi * 2 + j,
        )

    def hist_arrival(k, i, q):
        place = hist_in.at[k - 1, i, q]
        return remote(
            place, place, hist_s.at[k - 1, 0, q], hist_r.at[k - 1, i, q], section, sibling
        )

    load_mix.wait()
    position = lax.broadcasted_iota(jnp.int32, mix_v.shape, 1)

    def factors_of(s):
        return jnp.sum(jnp.where(position == s, mix_v[...], 0.0), axis=1, keepdims=True)

    factors = factors_of(section)
    plain = jnp.where(section == last, jnp.ones_like(factors[0:1]), factors[0:1])

    def finish(j, q):
        cross_copy(j, q).wait_recv()
        total = own_part[j, q] + x_in[j, q].astype(f32)
        past = x_res[j, :, pl.ds(pl.multiple_of(q * cols, cols), cols)].astype(f32)
        block = (past + total).astype(bf16)
        acc[...] = plain * block.astype(f32)
        for k in range(1, slots + 1):

            @pl.when(gets[k - 1])
            def _():
                hist_arrival(k, j, q).wait_recv()
                acc[...] += factors[k : k + 1] * hist_in[k - 1, j, q].astype(f32)

        mixed[j, q] = acc[...].astype(bf16)
        out_copy(j, q).start()

    def receive_block(j):
        for i in range(UNITS // 2):
            gather_copy(j, i).wait_recv()
            forward_copy(j, i).start()
        for i in range(UNITS // 2):
            forward_copy(j, i).wait_recv()

    for copy in loads:
        copy.wait()
    project_key_value(chip_rows, hi * 2 * rows)
    project_query(chip_rows, hi * 2 * rows)

    def out_weights_ready():
        for copy in out_loads:
            copy.wait()
        for c in range(DOTS):
            weight_copy(c).wait_recv()
        load_res.wait()
        residual_copy().wait_recv()

    def peer_block(j):
        target = ((1 - hi) * 2 + j) * rows
        return peer_rows.at[j], target

    @pl.when(hi == 0)
    def _():
        attend(0)
        attend(1)

    out_weights_ready()

    @pl.when(hi == 0)
    def _():
        for j in range(2):
            heads_copy(j).wait_recv()
            loop(DOTS, lambda c: own_output(j, j, c))

    @pl.when(late)
    def _():
        send_history()

    receive_block(0)
    project_key_value(*peer_block(0))
    project_query(*peer_block(0))

    @pl.when(hi == 0)
    def _():
        attend(2)
        heads_copy(2).wait_recv()
        loop(DOTS, lambda c: peer_output(2, 0, c))

    @pl.when(hi == 1)
    def _():
        attend(0)
        heads_copy(0).wait_recv()
        loop(DOTS, lambda c: peer_output(0, 0, c))

    receive_block(1)
    project_key_value(*peer_block(1))

    @pl.when(hi == 0)
    def _():
        finish(0, 0)

    @pl.when(hi == 1)
    def _():
        attend(2)

    project_query(*peer_block(1))

    @pl.when(hi == 0)
    def _():
        finish(0, 1)

        def after(p):
            @pl.when(p % 3 == 2)
            def _():
                finish(0, 2 + p // 3)

        attend(3, after)
        heads_copy(3).wait_recv()

        def step(c):
            peer_output(3, 1, c)
            finish(0, 4 + c)

        loop(DOTS, step)
        loop(CHUNKS, lambda q: finish(1, q))

    @pl.when(hi == 1)
    def _():
        heads_copy(2).wait_recv()

        def first(c):
            own_output(2, 0, c)
            loop(per_dot, lambda i: finish(0, c * per_dot + i))

        loop(DOTS // 2, first)
        attend(1)
        loop(DOTS // 2, lambda c: first(DOTS // 2 + c))
        heads_copy(1).wait_recv()
        loop(DOTS, lambda c: peer_output(1, 1, c))
        attend(3)
        heads_copy(3).wait_recv()

        def second(c):
            own_output(3, 1, c)
            loop(per_dot, lambda i: finish(1, c * per_dot + i))

        loop(DOTS, second)

    def out_arrival(c, q):
        place = out.at[0, :, pl.ds(pl.multiple_of(c * side + q * cols, cols), cols)]
        return remote(place, place, out_s.at[0, q], out_r.at[c, q], section, sibling)

    late_factors = factors_of(last)

    def take(q):
        for c in range(2):
            out_arrival(c, q).wait_recv()

            @pl.when(section == 0)
            def _():
                where = pl.ds(pl.multiple_of(c * side + q * cols, cols), cols)
                acc[...] = late_factors[0:1] * out[0, :, where].astype(f32)
                for k in range(1, slots + 1):

                    @pl.when(gets_last[k - 1])
                    def _():
                        hist_arrival(k, c, q).wait_recv()
                        acc[...] += late_factors[k : k + 1] * hist_in[k - 1, c, q].astype(f32)

                out[0, :, where] = acc[...].astype(bf16)

    loop(CHUNKS, take)

    for u in range(UNITS):
        sibling_copy(u).wait_send()
    for j in range(2):
        for i in range(UNITS // 2):
            gather_copy(j, i).wait_send()
            forward_copy(j, i).wait_send()
    for c in range(DOTS):
        weight_copy(c).wait_send()
    residual_copy().wait_send()
    for t in range(4):
        heads_copy(t).wait_send()
    for k in range(1, slots + 1):
        for to_last, sends in ((False, gives[k - 1]), (True, gives_last[k - 1])):

            @pl.when(sends)
            def _():
                def each(q, carry):
                    for c in range(2):
                        hist_copy(k, c, q, to_last).wait_send()
                    return carry

                lax.fori_loop(0, CHUNKS, each, 0)

    def drain(q):
        for j in range(2):
            cross_copy(j, q).wait_send()
            out_copy(j, q).wait_send()

    loop(CHUNKS, drain)


def solution(mesh):
    sections, tensor = mesh.shape["section"], mesh.shape["tensor"]
    assert tensor == 4

    def on_device(x, history, wq, wk, wv, wo, mix_weights):
        rows, width = x.shape[1:]
        slots = history.shape[1]
        q_width, kv_width = wq.shape[2], wk.shape[2]
        seq = rows * tensor
        tile = 2 * kv_width
        q_tiles = q_width // tile
        side = width // 2
        wide, cols = side // DOTS, side // CHUNKS
        bf16, f32 = jnp.bfloat16, jnp.float32
        dma = pltpu.SemaphoreType.DMA
        hbm = pl.BlockSpec(memory_space=pltpu.HBM)
        factors = mix_weights.T
        return pl.pallas_call(
            functools.partial(tick_kernel, sections),
            out_shape=pltpu.VMEM(x.shape, bf16),
            in_specs=[hbm] * 7,
            out_specs=pl.BlockSpec(memory_space=pltpu.VMEM),
            scratch_shapes=[
                pltpu.VMEM((rows, width), bf16),
                pltpu.VMEM((2, rows, side), bf16),
                pltpu.VMEM((2 * rows, width), bf16),
                pltpu.VMEM((2, rows, width), bf16),
                pltpu.VMEM((q_tiles + 1, width, tile), bf16),
                pltpu.VMEM((2, DOTS, q_width, wide), bf16),
                pltpu.VMEM((2 * q_tiles, seq, kv_width), bf16),
                pltpu.VMEM((4, seq, kv_width), bf16),
                pltpu.VMEM((4, seq, kv_width), bf16),
                pltpu.VMEM((4, 2, rows, q_width), bf16),
                pltpu.VMEM((2, CHUNKS, rows, cols), f32),
                pltpu.VMEM((2, CHUNKS, rows, cols), bf16),
                pltpu.VMEM((2, CHUNKS, rows, cols), bf16),
                pltpu.VMEM((2, CHUNKS, rows, cols), bf16),
                pltpu.VMEM((rows, cols), f32),
                pltpu.VMEM((slots, 2, CHUNKS, rows, cols), bf16),
                pltpu.VMEM(factors.shape, factors.dtype),
                dma((q_tiles + 2,)),
                dma((DOTS,)),
                dma,
                dma,
                dma,
                dma((slots, 2, CHUNKS)),
                dma((slots, 2, CHUNKS)),
                dma((UNITS,)),
                dma((UNITS,)),
                dma((2, UNITS // 2)),
                dma((2, UNITS // 2)),
                dma((2, UNITS // 2)),
                dma((2, UNITS // 2)),
                dma((DOTS,)),
                dma((DOTS,)),
                dma,
                dma,
                dma((4,)),
                dma((4,)),
                dma((2, CHUNKS)),
                dma((2, CHUNKS)),
                dma((2, CHUNKS)),
                dma((2, CHUNKS)),
            ],
            compiler_params=pltpu.CompilerParams(
                collective_id=0, has_side_effects=True, vmem_limit_bytes=56 * 1024 * 1024
            ),
        )(x, history, wq, wk, wv, wo, factors)

    placed = (
        P("section", "tensor", None),
        P("section", None, "tensor", None),
        P("section", None, "tensor"),
        P("section", None, "tensor"),
        P("section", None, "tensor"),
        P("section", "tensor", None),
        P(),
    )
    return jax.shard_map(
        on_device,
        mesh=mesh,
        in_specs=placed,
        out_specs=P("section", "tensor", None),
        check_vma=False,
    )
```

time: 79.7 us -> 70.9 us (0.89)
  Pallas kernels: 75.8 us -> 69.7 us
  local copies, waits for them, and re-layouts: 3.63 us -> 0.97 us
    pallas_call x1, Pallas kernels: 75.8 us -> 69.7 us  [on_device(): pl.pallas_call(functools.partial(tick_kernel, sections), out_shape=pltpu....]
    unnamed x2 -> x1, local copies, waits for them, and re-layouts: 3.63 us -> 0.97 us
where the time goes in v1:
time: 70.9 us; the launch traced here: 70.7 us
  Pallas kernels  69.7 us (98%)
  local copies, waits for them, and re-layouts  0.97 us (1%)
    pallas_call x1, Pallas kernels, on_device(): pl.pallas_call(functools.partial(tick_kernel, sections), out_shape=pltpu....  69.7 us

profile of v1, /device:TPU:31, one launch (start us, length us, event | category | flops | bytes accessed | tf_op | source)
XLA Modules:
  0.0 70.7 jit_solution(237842701248655133)
XLA Ops:
  0.0 69.7 %shard_map.73 = bf16[1,128,4096]{2,1,0:T(8,128)(2,1)S(1)} custom-call(bf16[1,128,4096]{2,1,0:T(8,128)(2,1)} %x_hbm.1, bf16[1,1,128,4096]{3,2,1,0:T(8,128)(2,1)} %hist_hbm.1, bf16[1,4096,768]{2,1,0:T(8,128)(2,1)} %wq_hbm.1, bf16[1,4096,128]{2,1,0:T(8,128)(2,1)} %wk_hbm.1, bf16[1,4096,128]{2,1,0:T(8,128)(2,1)} %wv_hbm.1, bf16[1,768,4096]{2,1,0:T(8,128)(2,1)} %wo_hbm.1, ...), custom_call_target="tpu_custom_call" | custom-call | tf_op jit(solution)/shard_map/pallas_call | solution.py:625
  69.7 1.0 %copy.9 = bf16[1,128,4096]{2,1,0:T(8,128)(2,1)} copy(bf16[1,128,4096]{2,1,0:T(8,128)(2,1)S(1)} %shard_map.73) | data formatting | bytes 2097152

commit v2 on v1

v2 whole, which is shorter than its diff:
```python
import functools
import math

import jax
import jax.numpy as jnp
from jax import lax
from jax.experimental import pallas as pl
from jax.experimental.pallas import tpu as pltpu
from jax.sharding import PartitionSpec as P

HEAD_DIM = 64
DILATION_STRIDE = 4
MESH = pl.DeviceIdType.MESH
UNITS = 8
DOTS = 4
CHUNKS = 16
PASTS = 4
PAIR = 2


def start(copy):
    copy.start()
    return copy


def tick_kernel(
    sections,
    x_hbm,
    hist_hbm,
    wq_hbm,
    wk_hbm,
    wv_hbm,
    wo_hbm,
    mix_hbm,
    out,
    x_own,
    x_res,
    chip_rows,
    peer_rows,
    w_all,
    w_out,
    q_all,
    k_pad,
    v_pad,
    heads,
    own_part,
    give,
    x_in,
    mixed,
    acc,
    hist_in,
    mix_v,
    w_sem,
    wo_sem,
    x_sem,
    res_sem,
    mix_sem,
    hist_s,
    hist_r,
    sib_s,
    sib_r,
    gx_s,
    gx_r,
    fw_s,
    fw_r,
    wr_s,
    wr_r,
    xr_s,
    xr_r,
    hd_s,
    hd_r,
    xs_s,
    xs_r,
    out_s,
    out_r,
    near_sem,
    far_sem,
):
    section = lax.axis_index("section")
    me = lax.axis_index("tensor")
    hi, lo = me // 2, me % 2
    sibling = hi * 2 + (1 - lo)
    peer = (1 - hi) * 2 + lo
    rows, width = x_own.shape
    slots = hist_in.shape[0]
    unit = rows // UNITS
    side = width // 2
    wide = side // DOTS
    cols = side // CHUNKS
    per_dot = CHUNKS // DOTS
    past = side // PASTS
    per_past = CHUNKS // PASTS
    q_tiles = w_all.shape[0] - 1
    tile = w_all.shape[2]
    half = tile // 2
    last = sections - 1
    nxt = lax.rem(section + 1, sections)
    prv = lax.rem(section + sections - 1, sections)
    f32, bf16 = jnp.float32, jnp.bfloat16

    middle = (section > 0) & (section < last)
    gets = [middle & (section >= DILATION_STRIDE * k) for k in range(1, slots + 1)]
    gets_last = [(section == 0) & (last >= DILATION_STRIDE * k) for k in range(1, slots + 1)]
    gives = [section + DILATION_STRIDE * k < last for k in range(1, slots + 1)]
    gives_last = [section + DILATION_STRIDE * k == last for k in range(1, slots + 1)]

    def load_unit(i):
        if i < 2:
            at = pl.ds(pl.multiple_of(order[i] * unit, unit), unit)
        else:
            at = pl.ds(2 * unit, rows - 2 * unit)
        return pltpu.make_async_copy(x_hbm.at[0, at], x_own.at[at], x_sem.at[i])

    order = [lo, 1 - lo] + list(range(2, UNITS))
    for i in range(3):
        load_unit(i).start()
    barrier = pltpu.get_barrier_semaphore()

    def greet(s, t):
        pl.semaphore_signal(
            barrier, inc=1, device_id={"section": s, "tensor": t}, device_id_type=MESH
        )

    host = hi == lo
    keeper = hi * 2 + (1 - hi)

    @pl.when(jnp.logical_not(host))
    def _():
        greet(section, sibling)
        greet(section, peer)

    greet(prv, keeper)
    expected = jnp.int32(2)
    for k in range(1, slots + 1):
        step = DILATION_STRIDE * k

        @pl.when(gets[k - 1])
        def _():
            greet(section - step, keeper)

        @pl.when(gets_last[k - 1])
        def _():
            greet(last - step, keeper)

        expected = expected + 2 * (gives[k - 1] | gives_last[k - 1]).astype(jnp.int32)

    loads = [
        pltpu.make_async_copy(
            wk_hbm.at[0], w_all.at[q_tiles, :, pl.ds(0, half)], w_sem
        ),
        pltpu.make_async_copy(
            wv_hbm.at[0], w_all.at[q_tiles, :, pl.ds(half, half)], w_sem
        ),
    ]
    for j in range(q_tiles):
        loads.append(
            pltpu.make_async_copy(
                wq_hbm.at[0, :, pl.ds(j * tile, tile)], w_all.at[j], w_sem
            )
        )
    for copy in loads:
        copy.start()
    load_mix = start(pltpu.make_async_copy(mix_hbm, mix_v, mix_sem))
    mine = pl.multiple_of(lo * rows, rows)
    my_side = pl.multiple_of(lo * side, side)
    other_side = pl.multiple_of((1 - lo) * side, side)

    def norm_unit(u):
        def norm_rows(i, carry):
            at = pl.multiple_of(u * unit + i * 16, 16)
            values = x_own[pl.ds(at, 16), :].astype(f32)
            inv = lax.rsqrt(jnp.mean(values * values, axis=-1, keepdims=True) + 1e-05)
            chip_rows[pl.ds(pl.multiple_of(mine + at, 16), 16), :] = (values * inv).astype(bf16)
            return carry

        lax.fori_loop(0, unit // 16, norm_rows, 0)

    def remote(src, dst, send, recv, s, t):
        return pltpu.make_async_remote_copy(
            src_ref=src,
            dst_ref=dst,
            send_sem=send,
            recv_sem=recv,
            device_id={"section": s, "tensor": t},
            device_id_type=MESH,
        )

    def settle(place, sem):
        return remote(place, place, sem, sem, section, sibling)

    def sibling_copy(u):
        place = chip_rows.at[pl.ds(pl.multiple_of(mine + u * unit, unit), unit)]
        return remote(place, place, sib_s, sib_r.at[u], section, sibling)

    def gather_copy(j, i):
        at = (2 * i + lo) * unit
        return remote(
            chip_rows.at[pl.ds(pl.multiple_of(j * rows + at, unit), unit)],
            peer_rows.at[j, pl.ds(pl.multiple_of(at, unit), unit)],
            gx_s,
            gx_r.at[j, i],
            section,
            peer,
        )

    def forward_copy(j, i):
        place = peer_rows.at[j, pl.ds(pl.multiple_of((2 * i + lo) * unit, unit), unit)]
        return remote(place, place, fw_s, fw_r.at[j], section, sibling)

    def hist_copy(k, c, q, to_last):
        src = hist_hbm.at[0, k - 1, :, pl.ds(pl.multiple_of(c * side + q * past, past), past)]
        slot = c if to_last else lo
        if to_last:
            s, t = 0, me
        else:
            s, t = section + DILATION_STRIDE * k, hi * 2 + c
        return remote(
            src,
            hist_in.at[k - 1, slot, q],
            hist_s.at[k - 1],
            hist_r.at[k - 1, slot, q],
            s,
            t,
        )

    def send_history():
        for k in range(1, slots + 1):
            for to_last, sends in ((False, gives[k - 1]), (True, gives_last[k - 1])):

                @pl.when(sends)
                def _():
                    def each(q, carry):
                        for c in range(2):
                            hist_copy(k, c, q, to_last).start()
                        return carry

                    lax.fori_loop(0, PASTS, each, 0)

    late = (lo == 1) & (section % 2 == 0)

    def tell(sem, t):
        pl.semaphore_signal(
            sem, inc=1, device_id={"section": section, "tensor": t}, device_id_type=MESH
        )

    load_unit(0).wait()
    norm_unit(order[0])

    @pl.when(host)
    def _():
        pl.semaphore_wait(barrier, 2)
        gather_copy(lo, 0).start()
        tell(near_sem, sibling)
        tell(near_sem, peer)
        sibling_copy(order[0]).start()

    load_unit(1).wait()
    norm_unit(order[1])

    @pl.when(jnp.logical_not(host))
    def _():
        pl.semaphore_wait(near_sem, 2)
        gather_copy(lo, 0).start()
        sibling_copy(order[0]).start()

    sibling_copy(order[1]).start()
    load_unit(2).wait()
    for i in range(2, UNITS):
        norm_unit(order[i])
        sibling_copy(order[i]).start()
        if i % 2 == 0:

            @pl.when(lo == 0)
            def _():
                gather_copy(0, i // 2).start()

    @pl.when(lo == 0)
    def _():
        for i in range(UNITS // 2):
            sibling_copy(2 * i).wait_recv()
            gather_copy(1, i).start()
        for i in range(UNITS // 2):
            sibling_copy(2 * i + 1).wait_recv()

    @pl.when(lo == 1)
    def _():
        for i in range(UNITS // 2):
            sibling_copy(2 * i + 1).wait_recv()
            gather_copy(0, i).start()
        for i in range(1, UNITS // 2):
            gather_copy(1, i).start()
        for i in range(UNITS // 2):
            sibling_copy(2 * i).wait_recv()

    @pl.when(jnp.logical_not(host))
    def _():
        pl.semaphore_wait(barrier, expected)
        tell(far_sem, sibling)

    @pl.when(host)
    def _():
        pl.semaphore_wait(far_sem, 1)

    @pl.when(jnp.logical_not(late))
    def _():
        send_history()

    def weight_copy(c):
        return remote(
            wo_hbm.at[0, :, pl.ds(pl.multiple_of(other_side + c * wide, wide), wide)],
            w_out.at[lo, c],
            wr_s,
            wr_r,
            section,
            sibling,
        )

    def residual_copy():
        return remote(
            x_own.at[:, pl.ds(other_side, side)], x_res.at[lo], xr_s, xr_r, section, sibling
        )

    for c in range(DOTS):
        pltpu.make_async_copy(
            wo_hbm.at[0, :, pl.ds(pl.multiple_of(my_side + c * wide, wide), wide)],
            w_out.at[lo, c],
            wo_sem,
        ).start()
        weight_copy(c).start()
    load_res = start(
        pltpu.make_async_copy(x_hbm.at[0, :, pl.ds(my_side, side)], x_res.at[lo], res_sem)
    )
    residual_copy().start()

    scale = 1.0 / math.sqrt(HEAD_DIM)

    def project_query(rows_ref, target, begin=0, end=None):
        size = rows_ref.shape[0]
        where = pl.ds(pl.multiple_of(target, size), size)

        def q_tile(j, carry):
            got = jnp.dot(rows_ref[...], w_all[j], preferred_element_type=f32)
            got = got.astype(bf16) * bf16(scale)
            q_all[2 * j, where, :] = got[:, :half]
            q_all[2 * j + 1, where, :] = got[:, half:]
            return carry

        lax.fori_loop(begin, q_tiles if end is None else end, q_tile, 0)

    def project_key_value(rows_ref, target):
        size = rows_ref.shape[0]
        where = pl.ds(pl.multiple_of(target, size), size)
        got = jnp.dot(rows_ref[...], w_all[q_tiles], preferred_element_type=f32)
        got = got.astype(bf16).astype(f32)
        for part, padded in ((got[:, :half], k_pad), (got[:, half:], v_pad)):
            lane = lax.broadcasted_iota(jnp.int32, part.shape, 1)
            turned = pltpu.roll(part, HEAD_DIM, 1)
            low = lane < HEAD_DIM
            zero = jnp.zeros_like(part)
            forms = (
                jnp.where(low, part, zero),
                jnp.where(low, zero, turned),
                jnp.where(low, turned, zero),
                jnp.where(low, zero, part),
            )
            for f, form in enumerate(forms):
                padded[f, where, :] = form.astype(bf16)

    pairs = q_all.shape[0]
    pairs_per_kv = pairs // (half // HEAD_DIM)

    def heads_copy(t):
        return remote(
            heads.at[t, lo], heads.at[t, lo], hd_s, hd_r.at[t], section, sibling
        )

    def attend(t, after=None):
        first, keys = t * rows, (t + 1) * rows
        seen = lax.broadcasted_iota(jnp.int32, (rows, rows), 0) >= lax.broadcasted_iota(
            jnp.int32, (rows, rows), 1
        )

        def group(kv, carry):
            chains = [(i, which) for i in range(pairs_per_kv) for which in range(2)]
            scores = []
            for i, which in chains:
                got = lax.dot_general(
                    q_all[kv * pairs_per_kv + i, first:keys, :],
                    k_pad[kv * 2 + which, :keys, :],
                    (((1,), (1,)), ((), ())),
                    preferred_element_type=f32,
                )
                scores.append((got[:, :first], jnp.where(seen, got[:, first:], -1e30)))
            probs = []
            for before, here in scores:
                top = jnp.max(here, axis=-1, keepdims=True)
                if first:
                    top = jnp.maximum(top, jnp.max(before, axis=-1, keepdims=True))
                here = jnp.exp(here - top)
                norm = jnp.sum(here, axis=-1, keepdims=True)
                if first:
                    before = jnp.exp(before - top)
                    norm = norm + jnp.sum(before, axis=-1, keepdims=True)
                inv = 1.0 / norm
                parts = [(here * inv).astype(bf16)]
                if first:
                    parts.insert(0, (before * inv).astype(bf16))
                probs.append(jnp.concatenate(parts, axis=1) if first else parts[0])
            terms = [
                jnp.dot(weights, v_pad[kv * 2 + which, :keys, :], preferred_element_type=f32)
                for weights, (i, which) in zip(probs, chains)
            ]
            for i in range(pairs_per_kv):
                total = terms[2 * i] + terms[2 * i + 1]
                at = pl.multiple_of((kv * pairs_per_kv + i) * half, half)
                heads[t, lo, :, pl.ds(at, half)] = total.astype(bf16)
            if after is not None:
                after(kv)
            return carry

        lax.fori_loop(0, pairs // pairs_per_kv, group, 0)
        heads_copy(t).start()

    def out_dot(t, c):
        got = jnp.dot(heads[t, 0], w_out[0, c], preferred_element_type=f32)
        return got + jnp.dot(heads[t, 1], w_out[1, c], preferred_element_type=f32)

    def cross_copy(j, q):
        span = PAIR if j == 0 else 1
        place = pl.ds(q, span)
        return remote(
            give.at[j, place], x_in.at[j, place], xs_s, xs_r.at[j, q], section, peer
        )

    def peer_output(t, j, c):
        got = out_dot(t, c).astype(bf16)
        span = PAIR if j == 0 else 1
        for i in range(per_dot):
            give[j, c * per_dot + i] = got[:, i * cols : (i + 1) * cols]
            if i % span == span - 1:
                cross_copy(j, c * per_dot + i - (span - 1)).start()

    def own_output(t, j, c):
        got = out_dot(t, c)
        for i in range(per_dot):
            own_part[j, c * per_dot + i] = got[:, i * cols : (i + 1) * cols]

    def loop(count, body):
        def step(i, carry):
            body(i)
            return carry

        lax.fori_loop(0, count, step, 0)

    def out_copy(j, q):
        return remote(
            mixed.at[j, q],
            out.at[0, :, pl.ds(pl.multiple_of(my_side + q * cols, cols), cols)],
            out_s,
            out_r.at[lo, q // PAIR],
            nxt,
            hi * 2 + j,
        )

    def hist_arrival(k, i, q):
        place = hist_in.at[k - 1, i, q]
        return remote(
            place, place, hist_s.at[k - 1], hist_r.at[k - 1, i, q], section, sibling
        )

    def history_of(k, i, q):
        @pl.when(q % per_past == 0)
        def _():
            hist_arrival(k, i, q // per_past).wait_recv()

        where = pl.ds(pl.multiple_of((q % per_past) * cols, cols), cols)
        return hist_in[k - 1, i, q // per_past, :, where].astype(f32)

    load_mix.wait()
    position = lax.broadcasted_iota(jnp.int32, mix_v.shape, 1)

    def factors_of(s):
        return jnp.sum(jnp.where(position == s, mix_v[...], 0.0), axis=1, keepdims=True)

    factors = factors_of(section)
    plain = jnp.where(section == last, jnp.ones_like(factors[0:1]), factors[0:1])

    def finish(j, q):
        if j == 0:

            @pl.when(q % PAIR == 0)
            def _():
                cross_copy(j, q).wait_recv()

        else:
            cross_copy(j, q).wait_recv()
        total = own_part[j, q] + x_in[j, q].astype(f32)
        given = x_res[j, :, pl.ds(pl.multiple_of(q * cols, cols), cols)].astype(f32)
        block = (given + total).astype(bf16)
        acc[...] = plain * block.astype(f32)
        for k in range(1, slots + 1):

            @pl.when(gets[k - 1])
            def _():
                acc[...] += factors[k : k + 1] * history_of(k, j, q)

        mixed[j, q] = acc[...].astype(bf16)
        out_copy(j, q).start()

    def receive_block(j, then=None):
        for i in range(UNITS // 2):
            gather_copy(j, i).wait_recv()
            forward_copy(j, i).start()
        if then is not None:
            then()
        settle(peer_rows.at[j, pl.ds(0, rows // 2)], fw_r.at[j]).wait_recv()

    pltpu.make_async_copy(w_all, w_all, w_sem).wait()
    project_key_value(chip_rows, hi * 2 * rows)
    project_query(chip_rows, hi * 2 * rows)

    def out_weights_ready():
        pltpu.make_async_copy(w_out.at[lo], w_out.at[lo], wo_sem).wait()
        settle(w_out.at[1 - lo], wr_r).wait_recv()
        load_res.wait()
        residual_copy().wait_recv()

    def peer_block(j):
        target = ((1 - hi) * 2 + j) * rows
        return peer_rows.at[j], target

    @pl.when(hi == 0)
    def _():
        attend(0)
        attend(1)

    out_weights_ready()

    @pl.when(hi == 0)
    def _():
        for j in range(2):
            heads_copy(j).wait_recv()
            loop(DOTS, lambda c: own_output(j, j, c))

    receive_block(0)
    project_key_value(*peer_block(0))
    project_query(*peer_block(0))

    @pl.when(hi == 0)
    def _():
        attend(2)
        heads_copy(2).wait_recv()
        loop(DOTS, lambda c: peer_output(2, 0, c))

    @pl.when(hi == 1)
    def _():
        attend(0)
        heads_copy(0).wait_recv()
        loop(DOTS, lambda c: peer_output(0, 0, c))

    @pl.when(late)
    def _():
        send_history()

    def finish_part(j, c, parts=2):
        count = CHUNKS // (parts * DOTS)
        loop(count, lambda i: finish(j, c * count + i))

    def first_part():
        @pl.when(hi == 0)
        def _():
            finish_part(0, 0)

    receive_block(1, first_part)
    project_key_value(*peer_block(1))

    @pl.when(hi == 1)
    def _():
        attend(2)

    project_query(*peer_block(1))

    @pl.when(hi == 0)
    def _():
        finish_part(0, 1)
        attend(3, lambda kv: finish_part(0, 2 + kv))
        finish_part(0, 4)
        heads_copy(3).wait_recv()

        def step(c):
            peer_output(3, 1, c)

            @pl.when(c > 0)
            def _():
                finish_part(0, 4 + c)

        loop(DOTS, step)
        loop(CHUNKS, lambda q: finish(1, q))

    @pl.when(hi == 1)
    def _():
        heads_copy(2).wait_recv()
        own_output(2, 0, 0)
        finish_part(0, 0, 1)
        attend(1)
        own_output(2, 0, 1)
        finish_part(0, 1, 1)
        heads_copy(1).wait_recv()

        def first(c):
            peer_output(1, 1, c)

            @pl.when(c < DOTS - 2)
            def _():
                own_output(2, 0, 2 + c)
                finish_part(0, 2 + c, 1)

        loop(DOTS, first)
        attend(3)
        heads_copy(3).wait_recv()

        def second(c):
            own_output(3, 1, c)
            finish_part(1, c, 1)

        loop(DOTS, second)

    def out_arrival(c, q):
        span = PAIR * cols
        place = out.at[0, :, pl.ds(pl.multiple_of(c * side + q * span, span), span)]
        return settle(place, out_r.at[c, q])

    late_factors = factors_of(last)

    def take(q):
        for c in range(2):
            out_arrival(c, q).wait_recv()

            @pl.when(section == 0)
            def _():
                for i in range(PAIR):
                    at = q * PAIR + i
                    where = pl.ds(pl.multiple_of(c * side + at * cols, cols), cols)
                    acc[...] = late_factors[0:1] * out[0, :, where].astype(f32)
                    for k in range(1, slots + 1):

                        @pl.when(gets_last[k - 1])
                        def _():
                            acc[...] += late_factors[k : k + 1] * history_of(k, c, at)

                    out[0, :, where] = acc[...].astype(bf16)

    loop(CHUNKS // PAIR, take)

    settle(chip_rows.at[pl.ds(0, rows)], sib_s).wait_send()
    settle(peer_rows.at[0], gx_s).wait_send()
    settle(peer_rows.at[0], fw_s).wait_send()
    settle(w_out.at[lo], wr_s).wait_send()
    residual_copy().wait_send()
    settle(heads.at[:, lo], hd_s).wait_send()
    for k in range(1, slots + 1):

        @pl.when(gives[k - 1] | gives_last[k - 1])
        def _():
            settle(hist_in.at[k - 1], hist_s.at[k - 1]).wait_send()

    settle(give, xs_s).wait_send()
    settle(mixed, out_s).wait_send()


def solution(mesh):
    sections, tensor = mesh.shape["section"], mesh.shape["tensor"]
    assert tensor == 4

    def on_device(x, history, wq, wk, wv, wo, mix_weights):
        rows, width = x.shape[1:]
        slots = history.shape[1]
        q_width, kv_width = wq.shape[2], wk.shape[2]
        seq = rows * tensor
        tile = 2 * kv_width
        q_tiles = q_width // tile
        side = width // 2
        wide, cols = side // DOTS, side // CHUNKS
        bf16, f32 = jnp.bfloat16, jnp.float32
        dma = pltpu.SemaphoreType.DMA
        hbm = pl.BlockSpec(memory_space=pltpu.HBM)
        factors = mix_weights.T
        return pl.pallas_call(
            functools.partial(tick_kernel, sections),
            out_shape=pltpu.VMEM(x.shape, bf16),
            in_specs=[hbm] * 7,
            out_specs=pl.BlockSpec(memory_space=pltpu.VMEM),
            scratch_shapes=[
                pltpu.VMEM((rows, width), bf16),
                pltpu.VMEM((2, rows, side), bf16),
                pltpu.VMEM((2 * rows, width), bf16),
                pltpu.VMEM((2, rows, width), bf16),
                pltpu.VMEM((q_tiles + 1, width, tile), bf16),
                pltpu.VMEM((2, DOTS, q_width, wide), bf16),
                pltpu.VMEM((2 * q_tiles, seq, kv_width), bf16),
                pltpu.VMEM((4, seq, kv_width), bf16),
                pltpu.VMEM((4, seq, kv_width), bf16),
                pltpu.VMEM((4, 2, rows, q_width), bf16),
                pltpu.VMEM((2, CHUNKS, rows, cols), f32),
                pltpu.VMEM((2, CHUNKS, rows, cols), bf16),
                pltpu.VMEM((2, CHUNKS, rows, cols), bf16),
                pltpu.VMEM((2, CHUNKS, rows, cols), bf16),
                pltpu.VMEM((rows, cols), f32),
                pltpu.VMEM((slots, 2, PASTS, rows, side // PASTS), bf16),
                pltpu.VMEM(factors.shape, factors.dtype),
                dma,
                dma,
                dma((3,)),
                dma,
                dma,
                dma((slots,)),
                dma((slots, 2, PASTS)),
                dma,
                dma((UNITS,)),
                dma,
                dma((2, UNITS // 2)),
                dma,
                dma((2,)),
                dma,
                dma,
                dma,
                dma,
                dma,
                dma((4,)),
                dma,
                dma((2, CHUNKS)),
                dma,
                dma((2, CHUNKS // PAIR)),
                pltpu.SemaphoreType.REGULAR,
                pltpu.SemaphoreType.REGULAR,
            ],
            compiler_params=pltpu.CompilerParams(
                collective_id=0, has_side_effects=True, vmem_limit_bytes=56 * 1024 * 1024
            ),
        )(x, history, wq, wk, wv, wo, factors)

    placed = (
        P("section", "tensor", None),
        P("section", None, "tensor", None),
        P("section", None, "tensor"),
        P("section", None, "tensor"),
        P("section", None, "tensor"),
        P("section", "tensor", None),
        P(),
    )
    return jax.shard_map(
        on_device,
        mesh=mesh,
        in_specs=placed,
        out_specs=P("section", "tensor", None),
        check_vma=False,
    )
```

time: 70.9 us -> 61.5 us (0.87)
  the two profiles are of different devices: /device:TPU:31 before, /device:TPU:3 now
where the time goes in v2:
time: 61.5 us; the launch traced here: 61.3 us
  Pallas kernels  60.4 us (98%)
  local copies, waits for them, and re-layouts  0.97 us (2%)
    pallas_call x1, Pallas kernels, on_device(): pl.pallas_call(functools.partial(tick_kernel, sections), out_shape=pltpu....  60.4 us

profile of v2, /device:TPU:3, one launch (start us, length us, event | category | flops | bytes accessed | tf_op | source)
XLA Modules:
  0.0 61.3 jit_solution(2242152859796973488)
XLA Ops:
  0.0 60.4 %shard_map.73 = bf16[1,128,4096]{2,1,0:T(8,128)(2,1)S(1)} custom-call(bf16[1,128,4096]{2,1,0:T(8,128)(2,1)} %x_hbm.1, bf16[1,1,128,4096]{3,2,1,0:T(8,128)(2,1)} %hist_hbm.1, bf16[1,4096,768]{2,1,0:T(8,128)(2,1)} %wq_hbm.1, bf16[1,4096,128]{2,1,0:T(8,128)(2,1)} %wk_hbm.1, bf16[1,4096,128]{2,1,0:T(8,128)(2,1)} %wv_hbm.1, bf16[1,768,4096]{2,1,0:T(8,128)(2,1)} %wo_hbm.1, ...), custom_call_target="tpu_custom_call" | custom-call | tf_op jit(solution)/shard_map/pallas_call | solution.py:688
  60.4 1.0 %copy.9 = bf16[1,128,4096]{2,1,0:T(8,128)(2,1)} copy(bf16[1,128,4096]{2,1,0:T(8,128)(2,1)S(1)} %shard_map.73) | data formatting | bytes 2097152

commit v3 on v2

--- a/solution.py
+++ b/solution.py
@@ -75,6 +75,7 @@
     out_r,
     near_sem,
     far_sem,
+    clear_sem,
 ):
     section = lax.axis_index("section")
     me = lax.axis_index("tensor")
@@ -190,10 +191,15 @@
 
     def sibling_copy(u):
         place = chip_rows.at[pl.ds(pl.multiple_of(mine + u * unit, unit), unit)]
-        return remote(place, place, sib_s, sib_r.at[u], section, sibling)
+        return remote(place, place, sib_s, sib_r, section, sibling)
+
+    share = UNITS // 2
+
+    def unit_of(i):
+        return UNITS - 2 if i == share else 2 * i + lo
 
     def gather_copy(j, i):
-        at = (2 * i + lo) * unit
+        at = unit_of(i) * unit
         return remote(
             chip_rows.at[pl.ds(pl.multiple_of(j * rows + at, unit), unit)],
             peer_rows.at[j, pl.ds(pl.multiple_of(at, unit), unit)],
@@ -204,7 +210,7 @@
         )
 
     def forward_copy(j, i):
-        place = peer_rows.at[j, pl.ds(pl.multiple_of((2 * i + lo) * unit, unit), unit)]
+        place = peer_rows.at[j, pl.ds(pl.multiple_of(unit_of(i) * unit, unit), unit)]
         return remote(place, place, fw_s, fw_r.at[j], section, sibling)
 
     def hist_copy(k, c, q, to_last):
@@ -274,23 +280,29 @@
             def _():
                 gather_copy(0, i // 2).start()
 
+    settle(chip_rows.at[pl.ds(0, rows)], sib_r).wait_recv()
+
     @pl.when(lo == 0)
     def _():
-        for i in range(UNITS // 2):
-            sibling_copy(2 * i).wait_recv()
+        for i in range(share - 1):
             gather_copy(1, i).start()
-        for i in range(UNITS // 2):
-            sibling_copy(2 * i + 1).wait_recv()
+
+        @pl.when(hi == 1)
+        def _():
+            gather_copy(1, share - 1).start()
 
     @pl.when(lo == 1)
     def _():
-        for i in range(UNITS // 2):
-            sibling_copy(2 * i + 1).wait_recv()
+        for i in range(share):
             gather_copy(0, i).start()
-        for i in range(1, UNITS // 2):
+        for i in range(1, share - 1):
             gather_copy(1, i).start()
-        for i in range(UNITS // 2):
-            sibling_copy(2 * i).wait_recv()
+
+        @pl.when(hi == 0)
+        def _():
+            gather_copy(1, share).start()
+
+        gather_copy(1, share - 1).start()
 
     @pl.when(jnp.logical_not(host))
     def _():
@@ -347,9 +359,8 @@
 
         lax.fori_loop(begin, q_tiles if end is None else end, q_tile, 0)
 
-    def project_key_value(rows_ref, target):
+    def project_key_value(rows_ref, first):
         size = rows_ref.shape[0]
-        where = pl.ds(pl.multiple_of(target, size), size)
         got = jnp.dot(rows_ref[...], w_all[q_tiles], preferred_element_type=f32)
         got = got.astype(bf16).astype(f32)
         for part, padded in ((got[:, :half], k_pad), (got[:, half:], v_pad)):
@@ -364,81 +375,86 @@
                 jnp.where(low, zero, part),
             )
             for f, form in enumerate(forms):
-                padded[f, where, :] = form.astype(bf16)
+                for i in range(size // rows):
+                    some = form[i * rows : (i + 1) * rows].astype(bf16)
+                    padded[f // 2, first + i, f % 2, :, :half] = some
+
+    def fill_ones():
+        low = lax.broadcasted_iota(jnp.int32, (rows, half), 1) < HEAD_DIM
+        for which in range(2):
+            ones = jnp.where(low == (which == 0), 1.0, 0.0).astype(bf16)
+            for kv in range(v_pad.shape[0]):
+                for i in range(v_pad.shape[1]):
+                    v_pad[kv, i, which, :, half:] = ones
 
     pairs = q_all.shape[0]
     pairs_per_kv = pairs // (half // HEAD_DIM)
 
-    def heads_copy(t):
-        return remote(
-            heads.at[t, lo], heads.at[t, lo], hd_s, hd_r.at[t], section, sibling
-        )
+    def heads_copy(t, kv):
+        span = pairs_per_kv * half
+        place = heads.at[t, lo, :, pl.ds(pl.multiple_of(kv * span, span), span)]
+        return remote(place, place, hd_s, hd_r.at[t], section, sibling)
+
+    def heads_ready(t):
+        settle(heads.at[t, 1 - lo], hd_r.at[t]).wait_recv()
 
     def attend(t, after=None):
-        first, keys = t * rows, (t + 1) * rows
+        first, blocks = t * rows, t + 1
         seen = lax.broadcasted_iota(jnp.int32, (rows, rows), 0) >= lax.broadcasted_iota(
             jnp.int32, (rows, rows), 1
         )
 
+        def exponents(scores, which):
+            mine = [
+                scores[:, (2 * i + which) * rows : (2 * i + which + 1) * rows]
+                for i in range(blocks)
+            ]
+            mine[t] = jnp.where(seen, mine[t], -1e30)
+            top = jnp.max(functools.reduce(jnp.maximum, mine), axis=-1, keepdims=True)
+            return [jnp.exp(part - top).astype(bf16) for part in mine]
+
         def group(kv, carry):
-            chains = [(i, which) for i in range(pairs_per_kv) for which in range(2)]
-            scores = []
-            for i, which in chains:
-                got = lax.dot_general(
-                    q_all[kv * pairs_per_kv + i, first:keys, :],
-                    k_pad[kv * 2 + which, :keys, :],
+            keys = k_pad[kv, :blocks].reshape(2 * blocks * rows, half)
+            values = v_pad[kv, :blocks].reshape(2 * blocks * rows, 2 * half)
+            scores = [
+                lax.dot_general(
+                    q_all[kv * pairs_per_kv + i, first : first + rows, :],
+                    keys,
                     (((1,), (1,)), ((), ())),
                     preferred_element_type=f32,
                 )
-                scores.append((got[:, :first], jnp.where(seen, got[:, first:], -1e30)))
+                for i in range(pairs_per_kv)
+            ]
             probs = []
-            for before, here in scores:
-                top = jnp.max(here, axis=-1, keepdims=True)
-                if first:
-                    top = jnp.maximum(top, jnp.max(before, axis=-1, keepdims=True))
-                here = jnp.exp(here - top)
-                norm = jnp.sum(here, axis=-1, keepdims=True)
-                if first:
-                    before = jnp.exp(before - top)
-                    norm = norm + jnp.sum(before, axis=-1, keepdims=True)
-                inv = 1.0 / norm
-                parts = [(here * inv).astype(bf16)]
-                if first:
-                    parts.insert(0, (before * inv).astype(bf16))
-                probs.append(jnp.concatenate(parts, axis=1) if first else parts[0])
-            terms = [
-                jnp.dot(weights, v_pad[kv * 2 + which, :keys, :], preferred_element_type=f32)
-                for weights, (i, which) in zip(probs, chains)
-            ]
-            for i in range(pairs_per_kv):
-                total = terms[2 * i] + terms[2 * i + 1]
+            for got in scores:
+                even, odd = exponents(got, 0), exponents(got, 1)
+                both = [part for pair in zip(even, odd) for part in pair]
+                probs.append(jnp.concatenate(both, axis=1))
+            for i, weights in enumerate(probs):
+                both = jnp.dot(weights, values, preferred_element_type=f32)
+                total = both[:, :half] / both[:, half:]
                 at = pl.multiple_of((kv * pairs_per_kv + i) * half, half)
                 heads[t, lo, :, pl.ds(at, half)] = total.astype(bf16)
+            heads_copy(t, kv).start()
             if after is not None:
                 after(kv)
             return carry
 
         lax.fori_loop(0, pairs // pairs_per_kv, group, 0)
-        heads_copy(t).start()
 
     def out_dot(t, c):
         got = jnp.dot(heads[t, 0], w_out[0, c], preferred_element_type=f32)
         return got + jnp.dot(heads[t, 1], w_out[1, c], preferred_element_type=f32)
 
     def cross_copy(j, q):
-        span = PAIR if j == 0 else 1
-        place = pl.ds(q, span)
-        return remote(
-            give.at[j, place], x_in.at[j, place], xs_s, xs_r.at[j, q], section, peer
-        )
-
-    def peer_output(t, j, c):
+        return remote(give.at[j, q], x_in.at[j, q], xs_s, xs_r.at[j, q], section, peer)
+
+    def peer_output(t, j, c, send=True):
         got = out_dot(t, c).astype(bf16)
-        span = PAIR if j == 0 else 1
         for i in range(per_dot):
             give[j, c * per_dot + i] = got[:, i * cols : (i + 1) * cols]
-            if i % span == span - 1:
-                cross_copy(j, c * per_dot + i - (span - 1)).start()
+            if send:
+                cross_copy(j, c * per_dot + i).start()
 
     def own_output(t, j, c):
         got = out_dot(t, c)
@@ -486,14 +502,7 @@
     plain = jnp.where(section == last, jnp.ones_like(factors[0:1]), factors[0:1])
 
     def finish(j, q):
-        if j == 0:
-
-            @pl.when(q % PAIR == 0)
-            def _():
-                cross_copy(j, q).wait_recv()
-
-        else:
-            cross_copy(j, q).wait_recv()
+        cross_copy(j, q).wait_recv()
         total = own_part[j, q] + x_in[j, q].astype(f32)
         given = x_res[j, :, pl.ds(pl.multiple_of(q * cols, cols), cols)].astype(f32)
         block = (given + total).astype(bf16)
@@ -508,15 +517,46 @@
         out_copy(j, q).start()
 
     def receive_block(j, then=None):
-        for i in range(UNITS // 2):
+        def pass_on(i):
             gather_copy(j, i).wait_recv()
             forward_copy(j, i).start()
-        if then is not None:
-            then()
-        settle(peer_rows.at[j, pl.ds(0, rows // 2)], fw_r.at[j]).wait_recv()
-
+
+        def passed(count):
+            settle(peer_rows.at[j, pl.ds(0, count * unit)], fw_r.at[j]).wait_recv()
+
+        if j == 0:
+            for i in range(share):
+                pass_on(i)
+            passed(share)
+            return
+        for i in range(share - 1):
+            pass_on(i)
+
+        @pl.when((hi == 1) & (lo == 1))
+        def _():
+            pass_on(share)
+
+        @pl.when((hi == 0) | (lo == 1))
+        def _():
+            pass_on(share - 1)
+
+        then()
+
+        @pl.when(hi == 0)
+        def _():
+            passed(share)
+
+        @pl.when((hi == 1) & (lo == 0))
+        def _():
+            passed(share + 1)
+
+        @pl.when((hi == 1) & (lo == 1))
+        def _():
+            passed(share - 1)
+
+    fill_ones()
     pltpu.make_async_copy(w_all, w_all, w_sem).wait()
-    project_key_value(chip_rows, hi * 2 * rows)
+    project_key_value(chip_rows, hi * 2)
     project_query(chip_rows, hi * 2 * rows)
 
     def out_weights_ready():
@@ -539,23 +579,38 @@
     @pl.when(hi == 0)
     def _():
         for j in range(2):
-            heads_copy(j).wait_recv()
+            heads_ready(j)
             loop(DOTS, lambda c: own_output(j, j, c))
 
     receive_block(0)
-    project_key_value(*peer_block(0))
+    project_key_value(peer_rows.at[0], (1 - hi) * 2)
     project_query(*peer_block(0))
 
     @pl.when(hi == 0)
     def _():
         attend(2)
-        heads_copy(2).wait_recv()
-        loop(DOTS, lambda c: peer_output(2, 0, c))
+
+        @pl.when(jnp.logical_not(host))
+        def _():
+            settle(peer_rows.at[0], gx_s).wait_send()
+            settle(peer_rows.at[0, pl.ds(0, unit)], gx_s).wait_send()
+            tell(clear_sem, sibling)
+            heads_ready(2)
+            loop(DOTS, lambda c: peer_output(2, 0, c))
+
+        @pl.when(host)
+        def _():
+            heads_ready(2)
+            loop(DOTS, lambda c: peer_output(2, 0, c, False))
+            settle(peer_rows.at[0, pl.ds(0, rows - unit)], gx_s).wait_send()
+            pl.semaphore_wait(clear_sem, 1)
+            loop(CHUNKS, lambda q: cross_copy(0, q).start())
+
 
     @pl.when(hi == 1)
     def _():
         attend(0)
-        heads_copy(0).wait_recv()
+        heads_ready(0)
         loop(DOTS, lambda c: peer_output(0, 0, c))
 
     @pl.when(late)
@@ -572,20 +627,15 @@
             finish_part(0, 0)
 
     receive_block(1, first_part)
-    project_key_value(*peer_block(1))
-
-    @pl.when(hi == 1)
-    def _():
-        attend(2)
-
-    project_query(*peer_block(1))
+    project_key_value(peer_rows.at[1], (1 - hi) * 2 + 1)
 
     @pl.when(hi == 0)
     def _():
+        project_query(*peer_block(1))
         finish_part(0, 1)
         attend(3, lambda kv: finish_part(0, 2 + kv))
         finish_part(0, 4)
-        heads_copy(3).wait_recv()
+        heads_ready(3)
 
         def step(c):
             peer_output(3, 1, c)
@@ -599,13 +649,16 @@
 
     @pl.when(hi == 1)
     def _():
-        heads_copy(2).wait_recv()
+        attend(2)
+        project_query(*peer_block(1), 0, q_tiles - 1)
+        heads_ready(2)
         own_output(2, 0, 0)
         finish_part(0, 0, 1)
+        project_query(*peer_block(1), q_tiles - 1, q_tiles)
         attend(1)
         own_output(2, 0, 1)
         finish_part(0, 1, 1)
-        heads_copy(1).wait_recv()
+        heads_ready(1)
 
         def first(c):
             peer_output(1, 1, c)
@@ -617,7 +670,7 @@
 
         loop(DOTS, first)
         attend(3)
-        heads_copy(3).wait_recv()
+        heads_ready(3)
 
         def second(c):
             own_output(3, 1, c)
@@ -653,8 +706,21 @@
     loop(CHUNKS // PAIR, take)
 
     settle(chip_rows.at[pl.ds(0, rows)], sib_s).wait_send()
-    settle(peer_rows.at[0], gx_s).wait_send()
-    settle(peer_rows.at[0], fw_s).wait_send()
+
+    @pl.when(hi == 1)
+    def _():
+        settle(peer_rows.at[0], gx_s).wait_send()
+
+    settle(peer_rows.at[0, pl.ds(0, rows - unit)], fw_s).wait_send()
+
+    @pl.when((hi == 0) | (lo == 1))
+    def _():
+        settle(peer_rows.at[0, pl.ds(0, unit)], fw_s).wait_send()
+
+    @pl.when((hi == 1) & (lo == 1))
+    def _():
+        settle(peer_rows.at[0, pl.ds(0, unit)], fw_s).wait_send()
+
     settle(w_out.at[lo], wr_s).wait_send()
     residual_copy().wait_send()
     settle(heads.at[:, lo], hd_s).wait_send()
@@ -698,8 +764,8 @@
                 pltpu.VMEM((q_tiles + 1, width, tile), bf16),
                 pltpu.VMEM((2, DOTS, q_width, wide), bf16),
                 pltpu.VMEM((2 * q_tiles, seq, kv_width), bf16),
-                pltpu.VMEM((4, seq, kv_width), bf16),
-                pltpu.VMEM((4, seq, kv_width), bf16),
+                pltpu.VMEM((kv_width // HEAD_DIM, tensor, 2, rows, kv_width), bf16),
+                pltpu.VMEM((kv_width // HEAD_DIM, tensor, 2, rows, 2 * kv_width), bf16),
                 pltpu.VMEM((4, 2, rows, q_width), bf16),
                 pltpu.VMEM((2, CHUNKS, rows, cols), f32),
                 pltpu.VMEM((2, CHUNKS, rows, cols), bf16),
@@ -716,9 +782,9 @@
                 dma((slots,)),
                 dma((slots, 2, PASTS)),
                 dma,
-                dma((UNITS,)),
-                dma,
-                dma((2, UNITS // 2)),
+                dma,
+                dma,
+                dma((2, UNITS // 2 + 1)),
                 dma,
                 dma((2,)),
                 dma,
@@ -731,6 +797,7 @@
                 dma((2, CHUNKS)),
                 dma,
                 dma((2, CHUNKS // PAIR)),
+                pltpu.SemaphoreType.REGULAR,
                 pltpu.SemaphoreType.REGULAR,
                 pltpu.SemaphoreType.REGULAR,
             ],

time: 61.5 us -> 60.9 us (level)
  Pallas kernels: 60.4 us -> 59.7 us
    pallas_call x1, Pallas kernels: 60.4 us -> 59.7 us  [on_device(): pl.pallas_call(functools.partial(tick_kernel, sections), out_shape=pltpu....]
where the time goes in v3:
time: 60.9 us; the launch traced here: 60.7 us
  Pallas kernels  59.7 us (98%)
  local copies, waits for them, and re-layouts  0.97 us (2%)
    pallas_call x1, Pallas kernels, on_device(): pl.pallas_call(functools.partial(tick_kernel, sections), out_shape=pltpu....  59.7 us

profile of v3, /device:TPU:3, one launch (start us, length us, event | category | flops | bytes accessed | tf_op | source)
XLA Modules:
  0.0 60.7 jit_solution(18087921287895933371)
XLA Ops:
  0.0 59.7 %shard_map.73 = bf16[1,128,4096]{2,1,0:T(8,128)(2,1)S(1)} custom-call(bf16[1,128,4096]{2,1,0:T(8,128)(2,1)} %x_hbm.1, bf16[1,1,128,4096]{3,2,1,0:T(8,128)(2,1)} %hist_hbm.1, bf16[1,4096,768]{2,1,0:T(8,128)(2,1)} %wq_hbm.1, bf16[1,4096,128]{2,1,0:T(8,128)(2,1)} %wk_hbm.1, bf16[1,4096,128]{2,1,0:T(8,128)(2,1)} %wv_hbm.1, bf16[1,768,4096]{2,1,0:T(8,128)(2,1)} %wo_hbm.1, ...), custom_call_target="tpu_custom_call" | custom-call | tf_op jit(solution)/shard_map/pallas_call | solution.py:754
  59.8 1.0 %copy.9 = bf16[1,128,4096]{2,1,0:T(8,128)(2,1)} copy(bf16[1,128,4096]{2,1,0:T(8,128)(2,1)S(1)} %shard_map.73) | data formatting | bytes 2097152

commit v4 on v3

--- a/solution.py
+++ b/solution.py
@@ -16,6 +16,7 @@
 CHUNKS = 16
 PASTS = 4
 PAIR = 2
+RELAYS = 1
 
 
 def start(copy):
@@ -73,6 +74,9 @@
     xs_r,
     out_s,
     out_r,
+    relay,
+    relay_s,
+    relay_r,
     near_sem,
     far_sem,
     clear_sem,
@@ -145,6 +149,22 @@
 
         expected = expected + 2 * (gives[k - 1] | gives_last[k - 1]).astype(jnp.int32)
 
+    vias = [max(last - 2 - r, 0) for r in range(RELAYS)]
+    sends_relay = (section == last) & (lo == 1)
+    does_relay = [(section == via) & (lo == 1) for via in vias]
+    expected = expected + RELAYS * (section == last).astype(jnp.int32)
+    for via, does in zip(vias, does_relay):
+
+        @pl.when(does)
+        def _():
+            greet(last, (1 - hi) * 2 + hi)
+
+        @pl.when(sends_relay)
+        def _():
+            greet(via, keeper)
+
+        expected = expected + (section == via).astype(jnp.int32)
+
     loads = [
         pltpu.make_async_copy(
             wk_hbm.at[0], w_all.at[q_tiles, :, pl.ds(0, half)], w_sem
@@ -243,6 +263,7 @@
                     lax.fori_loop(0, PASTS, each, 0)
 
     late = (lo == 1) & (section % 2 == 0)
+    latest = late & (section % DILATION_STRIDE == 0)
 
     def tell(sem, t):
         pl.semaphore_signal(
@@ -295,14 +316,17 @@
     def _():
         for i in range(share):
             gather_copy(0, i).start()
-        for i in range(1, share - 1):
+        for i in range(1, share - RELAYS):
             gather_copy(1, i).start()
 
         @pl.when(hi == 0)
         def _():
             gather_copy(1, share).start()
 
-        gather_copy(1, share - 1).start()
+        @pl.when(section < last)
+        def _():
+            for i in range(share - RELAYS, share):
+                gather_copy(1, i).start()
 
     @pl.when(jnp.logical_not(host))
     def _():
@@ -312,6 +336,21 @@
     @pl.when(host)
     def _():
         pl.semaphore_wait(far_sem, 1)
+
+    def relay_in(r):
+        src = chip_rows.at[pl.ds(2 * rows - (2 * r + 1) * unit, unit)]
+        return remote(src, relay.at[r], gx_s, relay_r.at[r], vias[r], peer)
+
+    def relay_out(r):
+        place = peer_rows.at[1, pl.ds(rows - (2 * r + 1) * unit, unit)]
+        return remote(
+            relay.at[r], place, relay_s.at[r], gx_r.at[1, share - 1 - r], last, me
+        )
+
+    @pl.when(sends_relay)
+    def _():
+        for r in range(RELAYS):
+            relay_in(r).start()
 
     @pl.when(jnp.logical_not(late))
     def _():
@@ -346,7 +385,7 @@
 
     scale = 1.0 / math.sqrt(HEAD_DIM)
 
-    def project_query(rows_ref, target, begin=0, end=None):
+    def project_query(rows_ref, target):
         size = rows_ref.shape[0]
         where = pl.ds(pl.multiple_of(target, size), size)
 
@@ -357,7 +396,7 @@
             q_all[2 * j + 1, where, :] = got[:, half:]
             return carry
 
-        lax.fori_loop(begin, q_tiles if end is None else end, q_tile, 0)
+        lax.fori_loop(0, q_tiles, q_tile, 0)
 
     def project_key_value(rows_ref, first):
         size = rows_ref.shape[0]
@@ -461,6 +500,15 @@
         for i in range(per_dot):
             own_part[j, c * per_dot + i] = got[:, i * cols : (i + 1) * cols]
 
+    def own_half(t, j, c, core):
+        got = jnp.dot(heads[t, core], w_out[core, c], preferred_element_type=f32)
+        for i in range(per_dot):
+            part = got[:, i * cols : (i + 1) * cols]
+            if core is lo:
+                own_part[j, c * per_dot + i] = part
+            else:
+                own_part[j, c * per_dot + i] += part
+
     def loop(count, body):
         def step(i, carry):
             body(i)
@@ -582,6 +630,13 @@
             heads_ready(j)
             loop(DOTS, lambda c: own_output(j, j, c))
 
+    for r in range(RELAYS):
+
+        @pl.when(does_relay[r])
+        def _():
+            relay_in(r).wait_recv()
+            relay_out(r).start()
+
     receive_block(0)
     project_key_value(peer_rows.at[0], (1 - hi) * 2)
     project_query(*peer_block(0))
@@ -613,7 +668,7 @@
         heads_ready(0)
         loop(DOTS, lambda c: peer_output(0, 0, c))
 
-    @pl.when(late)
+    @pl.when(late & jnp.logical_not(latest))
     def _():
         send_history()
 
@@ -634,6 +689,11 @@
         project_query(*peer_block(1))
         finish_part(0, 1)
         attend(3, lambda kv: finish_part(0, 2 + kv))
+
+        @pl.when(latest)
+        def _():
+            send_history()
+
         finish_part(0, 4)
         heads_ready(3)
 
@@ -650,13 +710,18 @@
     @pl.when(hi == 1)
     def _():
         attend(2)
-        project_query(*peer_block(1), 0, q_tiles - 1)
+        loop(DOTS, lambda c: own_half(2, 0, c, lo))
         heads_ready(2)
-        own_output(2, 0, 0)
+        own_half(2, 0, 0, 1 - lo)
         finish_part(0, 0, 1)
-        project_query(*peer_block(1), q_tiles - 1, q_tiles)
+        project_query(*peer_block(1))
         attend(1)
-        own_output(2, 0, 1)
+
+        @pl.when(latest)
+        def _():
+            send_history()
+
+        own_half(2, 0, 1, 1 - lo)
         finish_part(0, 1, 1)
         heads_ready(1)
 
@@ -665,7 +730,7 @@
 
             @pl.when(c < DOTS - 2)
             def _():
-                own_output(2, 0, 2 + c)
+                own_half(2, 0, 2 + c, 1 - lo)
                 finish_part(0, 2 + c, 1)
 
         loop(DOTS, first)
@@ -732,6 +797,12 @@
 
     settle(give, xs_s).wait_send()
     settle(mixed, out_s).wait_send()
+
+    for r in range(RELAYS):
+
+        @pl.when(does_relay[r])
+        def _():
+            relay_out(r).wait_send()
 
 
 def solution(mesh):
@@ -797,6 +868,9 @@
                 dma((2, CHUNKS)),
                 dma,
                 dma((2, CHUNKS // PAIR)),
+                pltpu.VMEM((RELAYS, rows // UNITS, width), bf16),
+                dma((RELAYS,)),
+                dma((RELAYS,)),
                 pltpu.SemaphoreType.REGULAR,
                 pltpu.SemaphoreType.REGULAR,
                 pltpu.SemaphoreType.REGULAR,

time: 60.9 us -> 59.5 us (0.977)
  Pallas kernels: 59.7 us -> 58.4 us
    pallas_call x1, Pallas kernels: 59.7 us -> 58.4 us  [on_device(): pl.pallas_call(functools.partial(tick_kernel, sections), out_shape=pltpu....]
where the time goes in v4:
time: 59.5 us; the launch traced here: 59.4 us
  Pallas kernels  58.4 us (98%)
  local copies, waits for them, and re-layouts  0.97 us (2%)
    pallas_call x1, Pallas kernels, on_device(): pl.pallas_call(functools.partial(tick_kernel, sections), out_shape=pltpu....  58.4 us

profile of v4, /device:TPU:3, one launch (start us, length us, event | category | flops | bytes accessed | tf_op | source)
XLA Modules:
  0.0 59.4 jit_solution(13453542081235033597)
XLA Ops:
  0.0 58.4 %shard_map.73 = bf16[1,128,4096]{2,1,0:T(8,128)(2,1)S(1)} custom-call(bf16[1,128,4096]{2,1,0:T(8,128)(2,1)} %x_hbm.1, bf16[1,1,128,4096]{3,2,1,0:T(8,128)(2,1)} %hist_hbm.1, bf16[1,4096,768]{2,1,0:T(8,128)(2,1)} %wq_hbm.1, bf16[1,4096,128]{2,1,0:T(8,128)(2,1)} %wk_hbm.1, bf16[1,4096,128]{2,1,0:T(8,128)(2,1)} %wv_hbm.1, bf16[1,768,4096]{2,1,0:T(8,128)(2,1)} %wo_hbm.1, ...), custom_call_target="tpu_custom_call" | custom-call | tf_op jit(solution)/shard_map/pallas_call | solution.py:825
  58.4 1.0 %copy.9 = bf16[1,128,4096]{2,1,0:T(8,128)(2,1)} copy(bf16[1,128,4096]{2,1,0:T(8,128)(2,1)S(1)} %shard_map.73) | data formatting | bytes 2097152

commit v5 on v4

--- a/solution.py
+++ b/solution.py
@@ -710,31 +710,35 @@
     @pl.when(hi == 1)
     def _():
         attend(2)
-        loop(DOTS, lambda c: own_half(2, 0, c, lo))
+        own_half(2, 0, 0, lo)
+
+        @pl.when(lo == 1)
+        def _():
+            project_query(*peer_block(1))
+
         heads_ready(2)
         own_half(2, 0, 0, 1 - lo)
         finish_part(0, 0, 1)
-        project_query(*peer_block(1))
+
+        @pl.when(lo == 0)
+        def _():
+            project_query(*peer_block(1))
+
         attend(1)
 
         @pl.when(latest)
         def _():
             send_history()
 
-        own_half(2, 0, 1, 1 - lo)
+        own_output(2, 0, 1)
         finish_part(0, 1, 1)
         heads_ready(1)
-
-        def first(c):
-            peer_output(1, 1, c)
-
-            @pl.when(c < DOTS - 2)
-            def _():
-                own_half(2, 0, 2 + c, 1 - lo)
-                finish_part(0, 2 + c, 1)
-
-        loop(DOTS, first)
+        loop(DOTS, lambda c: peer_output(1, 1, c))
+        own_output(2, 0, 2)
+        finish_part(0, 2, 1)
         attend(3)
+        own_output(2, 0, 3)
+        finish_part(0, 3, 1)
         heads_ready(3)
 
         def second(c):

time: 59.5 us -> 58.9 us (0.990)
  Pallas kernels: 58.4 us -> 57.7 us
    pallas_call x1, Pallas kernels: 58.4 us -> 57.7 us  [on_device(): pl.pallas_call(functools.partial(tick_kernel, sections), out_shape=pltpu....]
where the time goes in v5:
time: 58.9 us; the launch traced here: 58.7 us
  Pallas kernels  57.7 us (98%)
  local copies, waits for them, and re-layouts  0.97 us (2%)
    pallas_call x1, Pallas kernels, on_device(): pl.pallas_call(functools.partial(tick_kernel, sections), out_shape=pltpu....  57.7 us

profile of v5, /device:TPU:3, one launch (start us, length us, event | category | flops | bytes accessed | tf_op | source)
XLA Modules:
  0.0 58.7 jit_solution(2581873534726628554)
XLA Ops:
  0.0 57.7 %shard_map.73 = bf16[1,128,4096]{2,1,0:T(8,128)(2,1)S(1)} custom-call(bf16[1,128,4096]{2,1,0:T(8,128)(2,1)} %x_hbm.1, bf16[1,1,128,4096]{3,2,1,0:T(8,128)(2,1)} %hist_hbm.1, bf16[1,4096,768]{2,1,0:T(8,128)(2,1)} %wq_hbm.1, bf16[1,4096,128]{2,1,0:T(8,128)(2,1)} %wk_hbm.1, bf16[1,4096,128]{2,1,0:T(8,128)(2,1)} %wv_hbm.1, bf16[1,768,4096]{2,1,0:T(8,128)(2,1)} %wo_hbm.1, ...), custom_call_target="tpu_custom_call" | custom-call | tf_op jit(solution)/shard_map/pallas_call | solution.py:829
  57.7 1.0 %copy.9 = bf16[1,128,4096]{2,1,0:T(8,128)(2,1)} copy(bf16[1,128,4096]{2,1,0:T(8,128)(2,1)S(1)} %shard_map.73) | data formatting | bytes 2097152

commit v6 on v5

--- a/solution.py
+++ b/solution.py
@@ -15,7 +15,7 @@
 DOTS = 4
 CHUNKS = 16
 PASTS = 4
-PAIR = 2
+PAIR = 4
 RELAYS = 1
 
 

time: 58.9 us -> 58.9 us (level)
  no operation moved by 1% of the time
where the time goes in v6:
time: 58.9 us; the launch traced here: 58.7 us
  Pallas kernels  57.7 us (98%)
  local copies, waits for them, and re-layouts  0.97 us (2%)
    pallas_call x1, Pallas kernels, on_device(): pl.pallas_call(functools.partial(tick_kernel, sections), out_shape=pltpu....  57.7 us

profile of v6, /device:TPU:3, one launch (start us, length us, event | category | flops | bytes accessed | tf_op | source)
XLA Modules:
  0.0 58.7 jit_solution(10604857235478000092)
XLA Ops:
  0.0 57.7 %shard_map.73 = bf16[1,128,4096]{2,1,0:T(8,128)(2,1)S(1)} custom-call(bf16[1,128,4096]{2,1,0:T(8,128)(2,1)} %x_hbm.1, bf16[1,1,128,4096]{3,2,1,0:T(8,128)(2,1)} %hist_hbm.1, bf16[1,4096,768]{2,1,0:T(8,128)(2,1)} %wq_hbm.1, bf16[1,4096,128]{2,1,0:T(8,128)(2,1)} %wk_hbm.1, bf16[1,4096,128]{2,1,0:T(8,128)(2,1)} %wv_hbm.1, bf16[1,768,4096]{2,1,0:T(8,128)(2,1)} %wo_hbm.1, ...), custom_call_target="tpu_custom_call" | custom-call | tf_op jit(solution)/shard_map/pallas_call | solution.py:829
  57.7 1.0 %copy.9 = bf16[1,128,4096]{2,1,0:T(8,128)(2,1)} copy(bf16[1,128,4096]{2,1,0:T(8,128)(2,1)S(1)} %shard_map.73) | data formatting | bytes 2097152
